TPU v7x, 32 devices: a whole 2x2x4 slice. The times are simulated.
32 devices in a mesh: group: 2 (over y), plane: 4 (over z), planey: 2 (over x), ens: 2 (over core).
Axes of the slice: x: 2, y: 2, z: 4, core: 2. Of those that a mesh axis runs over, the one named last changes fastest.
Arguments:
- u_prior: float32 [8, 2, 10, 64, 256], P(('group', 'ens'), None, None, 'plane', 'planey'), parts along dimension 0, may hold values from -6 to 6
- friction_rows: int32 [8], P(('group', 'ens')), parts along dimension 0, may hold values from 0 to 15
- friction_table: float32 [32, 64, 256], P('group', 'plane', 'planey'), parts along dimension 0, may hold values from 0.3 to 3
- bed_fixed: int32 [64, 256], P('plane', 'planey'), may hold values from -536870912 to 536870911
- ice_mask: int32 [64, 256], P('plane', 'planey'), may hold values 0 or 1
Outputs:
- mean_velocity: float32 [4, 10, 64, 256], P('group', None, 'plane', 'planey'), parts along dimension 0
There are 2 independent parts, one for each index of `group`. A program takes and returns all parts, laid end to end along the dimension named above; an argument that names none is the same for every part. Nothing has to cross between parts.
Inputs may be any that keep to these rules, and one draw needn't show every extreme that they name: `friction_rows`: each sample names one row of the friction table.
All inputs are finite; a program needn't handle non-finite values. No bound on the sum of `ice_mask` on one device may be relied on, other than what follows from the above.
Results may differ from a plain program's by a relative error of at most 0.0003.
Values sent between devices are 32-bit elements; how exact they have to be, the bound alone decides.
A program may use at most 64 MiB of HBM per device.

v0:
```python
import functools
import jax
import jax.numpy as jnp
from jax import lax
from jax.experimental import pallas as pl
from jax.experimental.pallas import tpu as pltpu
from jax.sharding import PartitionSpec as P

bed_unit = 2.0 ** (-29)
HALO = 4
SLOTS = 16
STEP_I = (0.25, 0.125)
STEP_J = (0.125, 0.25)


def iota(shape, dim):
    return lax.broadcasted_iota(jnp.int32, shape, dim)


def shift_i(x, step):
    return pltpu.roll(x, (-step) % x.shape[-2], x.ndim - 2)


def shift_j(x, step):
    rolled = pltpu.roll(x, (-step) % x.shape[-1], x.ndim - 1)
    swapped = jnp.concatenate([rolled[1:2], rolled[0:1]], axis=0)
    lane = iota(x.shape, x.ndim - 1)
    edge = 0 if step < 0 else x.shape[-1] - 1
    return jnp.where(lane == edge, swapped, rolled)


def spread_ij(x, c):
    x = x + STEP_I[c] * (shift_i(x, 1) + shift_i(x, -1))
    return x + STEP_J[c] * (shift_j(x, 1) + shift_j(x, -1))


def spread_z(ref, index, z):
    return ref[index + (z + 1,)] + 0.5 * (ref[index + (z,)] + ref[index + (z + 2,)])


def chunk_places(members, layers):
    chunks, places, pair, group = [], [], 0, 0
    for m in range(members):
        base = 2 + members if m == 0 else 0
        base_even = base + base % 2
        count = base_even + 2 * layers
        pairs, groups = count // 2, (count + SLOTS - 1) // SLOTS
        chunks.append((pair, pairs, group, groups))
        places.append(base_even)
        pair, group = pair + pairs, group + groups
    return chunks, places


def kernel(sizes, rows_hbm, u_hbm, table_hbm, bed_hbm, mask_hbm, out_ref,
           rows_ref, u_v, table_v, bed_v, mask_v,
           up_s, down_s, side_s, corner_s,
           below_r, above_r, side_r, corner_r, hx,
           ext, roots, tr, pa, pb, r_ext, a_ext, force,
           r_core, a_core, w_core, r_peer, a_peer, w_peer,
           gram_s, gram_r,
           relay, in_sem, halo_send, halo_recv, peer_send, peer_recv, gram_send, gram_recv):
    np_, nq, ne = sizes
    members, _, layers, rows, cols = u_v.shape
    ring = rows + 2 * HALO
    ix, iy, ie = lax.axis_index("plane"), lax.axis_index("planey"), lax.axis_index("ens")

    total = np_ * nq * ne
    mesh_id = pl.DeviceIdType.MESH

    adjacent = []
    for dx in (0, -1, 1):
        for dy in (0, -1, 1):
            for de in range(ne):
                if (dx, dy, de) == (0, 0, 0):
                    continue
                tx, ty = ix + dx, iy + dy
                ok = (tx >= 0) & (tx < np_) & (ty >= 0) & (ty < nq)
                where = {"plane": jnp.clip(tx, 0, np_ - 1), "planey": jnp.clip(ty, 0, nq - 1),
                         "ens": lax.rem(ie + de, ne)}
                adjacent.append((ok, where))
    span_x = 1 + (ix > 0).astype(jnp.int32) + (ix < np_ - 1).astype(jnp.int32)
    span_y = 1 + (iy > 0).astype(jnp.int32) + (iy < nq - 1).astype(jnp.int32)
    adjacent_count = span_x * span_y * ne - 1
    rounds = max(max(np_, nq) - 2, 0)

    def signal_adjacent(sem):
        for ok, where in adjacent:
            @pl.when(ok)
            def _(where=where):
                pl.semaphore_signal(sem, inc=1, device_id=where, device_id_type=mesh_id)

    barrier = pltpu.get_barrier_semaphore()
    signal_adjacent(barrier)

    loads = [
        pltpu.make_async_copy(src, dst, in_sem.at[i])
        for i, (src, dst) in enumerate(
            ((u_hbm, u_v), (table_hbm, table_v), (bed_hbm, bed_v), (mask_hbm, mask_v),
             (rows_hbm, rows_ref))
        )
    ]
    for load in loads:
        load.start()

    def group_target(d):
        de, rest = d // (np_ * nq), d % (np_ * nq)
        return {
            "plane": lax.rem(ix + rest // nq, np_),
            "planey": lax.rem(iy + rest % nq, nq),
            "ens": lax.rem(ie + de, ne),
        }

    def each_peer(fn):
        if total <= 32:
            for d in range(1, total):
                fn(d)
        else:
            def step(d, carry):
                fn(d)
                return carry
            lax.fori_loop(1, total, step, 0)

    shared = [
        lambda: bed_v[...].astype(jnp.float32) * bed_unit,
        lambda: mask_v[...].astype(jnp.float32),
    ] + [(lambda m=m: table_v[rows_ref[m]]) for m in range(members)]
    if len(shared) % 2:
        shared.append(shared[-1])
    chunks, places = chunk_places(members, layers)
    readers = [
        (shared if m == 0 else [])
        + [(lambda m=m, c=c, z=z: u_v[m, c, z]) for z in range(layers) for c in range(2)]
        for m in range(members)
    ]

    flows = [[] for _ in chunks]
    absent = []
    for i, (dx, dy, src, dst) in enumerate((
        (-1, 0, up_s, below_r),
        (1, 0, down_s, above_r),
        (0, -1, side_s, side_r.at[1]),
        (0, 1, side_s, side_r.at[0]),
        (-1, -1, corner_s, corner_r.at[0, 1]),
        (-1, 1, corner_s, corner_r.at[0, 0]),
        (1, -1, corner_s, corner_r.at[1, 1]),
        (1, 1, corner_s, corner_r.at[1, 0]),
    )):
        tx, ty = ix + dx, iy + dy
        sx, sy = ix - dx, iy - dy
        to_ok = (tx >= 0) & (tx < np_) & (ty >= 0) & (ty < nq)
        from_ok = (sx >= 0) & (sx < np_) & (sy >= 0) & (sy < nq)
        absent.append((jnp.logical_not(from_ok), dst))
        for k, (pair, pairs, group, groups) in enumerate(chunks):
            part = pl.ds(pair, pairs) if i < 2 else pl.ds(group, groups)
            copy = pltpu.make_async_remote_copy(
                src_ref=src.at[part], dst_ref=dst.at[part],
                send_sem=halo_send.at[8 * k + i], recv_sem=halo_recv.at[8 * k + i],
                device_id={"plane": jnp.clip(tx, 0, np_ - 1), "planey": jnp.clip(ty, 0, nq - 1)},
                device_id_type=mesh_id)
            flows[k].append((copy, to_ok, from_ok))

    for load in loads:
        load.wait()

    low8 = iota((8, cols), 0) < 4
    lane_x = iota((rows, cols), 1)

    def ends(value):
        return jnp.where(low8, value[0:8], value[rows - 8:rows])

    for (pair, pairs, group, groups), read in zip(chunks, readers):
        for g in range(groups):
            packed = jnp.zeros((rows, cols), jnp.float32)
            for k in range(min(SLOTS, len(read) - g * SLOTS)):
                rolled = pltpu.roll(read[g * SLOTS + k](), (8 * k + 4) % cols, 1)
                packed = jnp.where((lane_x // 8) == k, rolled, packed)
            side_s[group + g] = packed
            corner_s[group + g] = ends(packed)
        for i in range(pairs):
            first = ends(read[2 * i]())
            turned = pltpu.roll(ends(read[min(2 * i + 1, len(read) - 1)]()), 4, 0)
            up_s[pair + i] = jnp.where(low8, first, turned)
            down_s[pair + i] = jnp.where(low8, turned, first)

    pl.semaphore_wait(barrier, adjacent_count)
    for chunk in flows:
        for copy, to_ok, from_ok in chunk:
            pl.when(to_ok)(copy.start)
    if rounds > 0:
        signal_adjacent(relay.at[0])

    for gone, dst in absent:
        @pl.when(gone)
        def _(dst=dst):
            dst[...] = jnp.zeros(dst.shape, jnp.float32)
    zero = jnp.zeros((2, ring, cols), jnp.float32)
    for m in range(members):
        for end in (0, layers + 1):
            roots[m, end] = zero
            for c in range(2):
                ext[m, c, end] = zero
                pa[m, c, end] = zero
                pb[m, c, end] = zero
    cover_core = mask_v[...].astype(jnp.float32)
    for c in range(2):
        for z in range(layers):
            summed = u_v[0, c, z]
            for m in range(1, members):
                summed = summed + u_v[m, c, z]
            w_core[c, z] = cover_core * summed

    def arrive(k):
        for copy, to_ok, from_ok in flows[k]:
            pl.when(from_ok)(copy.wait_recv)
        _, _, group, groups = chunks[k]
        for g in range(group, group + groups):
            hx[g, 0:rows] = jnp.where(lane_x % 8 < 4, side_r[0, g], side_r[1, g])
            left = jnp.where(low8, corner_r[0, 0, g], corner_r[1, 0, g])
            right = jnp.where(low8, corner_r[0, 1, g], corner_r[1, 1, g])
            hx[g, rows:ring] = jnp.where(lane_x[0:8] % 8 < 4, left, right)

    def extended(k, p):
        pair, _, group, _ = chunks[k]
        i = pair + p // 2
        if p % 2 == 0:
            tail = jnp.where(low8, below_r[i], above_r[i])
        else:
            tail = pltpu.roll(jnp.where(low8, above_r[i], below_r[i]), 4, 0)
        core = jnp.concatenate([readers[k][p](), tail], axis=0)
        halo = pltpu.roll(hx[group + p // SLOTS], (-(8 * (p % SLOTS) + 4)) % cols, 1)
        return jnp.stack([core, halo])

    def assemble(m):
        arrive(m)
        base = places[m]
        for z in range(layers):
            for c in range(2):
                ext[m, c, z + 1] = extended(m, base + 2 * z + c)
        if m > 0:
            return
        bed = extended(0, 0)
        cover = extended(0, 1)
        row = iota((2, ring, cols), 1)
        position = (ix * rows + jnp.where(row < rows + HALO, row, row - ring)).astype(jnp.float32)
        thickness = 1.0 + 2.0 * position / (np_ * rows - 1)
        slope_x = (shift_i(bed, 1) - shift_i(bed, -1)) * 0.5
        slope_y = (shift_j(bed, 1) - shift_j(bed, -1)) * 0.5
        force[0] = -(cover * thickness * slope_x)
        force[1] = -(cover * thickness * slope_y)
        force[2] = cover
        force[3 + members] = 2.0 * cover
        for k in range(members):
            force[3 + k] = cover * extended(0, 2 + k)

    def roots_step(m, z):
        u, v = ext[m, 0, z + 1], ext[m, 1, z + 1]
        u_i = (shift_i(u, 1) - shift_i(u, -1)) * 0.5
        v_j = (shift_j(v, 1) - shift_j(v, -1)) * 0.5
        shear = ((shift_j(u, 1) - shift_j(u, -1)) + (shift_i(v, 1) - shift_i(v, -1))) * 0.5
        u_z = (ext[m, 0, z + 2] - ext[m, 0, z]) * 0.5
        v_z = (ext[m, 1, z + 2] - ext[m, 1, z]) * 0.5
        strain = (u_i * u_i + v_j * v_j + u_i * v_j + 0.25 * shear * shear
                  + 0.25 * (u_z * u_z + v_z * v_z))
        root = force[3 + members] * jnp.exp(jnp.log(strain + 0.1) * (-1.0 / 6.0))
        roots[m, z + 1] = root
        pa[m, 0, z + 1] = root * u
        pa[m, 1, z + 1] = root * v

    def image(m, c, z, field, p_ref):
        spread = spread_ij(spread_z(p_ref, (m, c), z), c)
        return tr[m, c, z] * field - roots[m, z + 1] * spread

    def residual_step(m, z, acc):
        near = spread_z(roots, (m,), z)
        diag = 1.0 - force[2]
        if z == 0:
            diag = diag + force[3 + m]
        for c in range(2):
            tr[m, c, z] = roots[m, z + 1] * spread_ij(near, c) + diag
            r = force[c] - image(m, c, z, force[2] * ext[m, c, z + 1], pa)
            r_ext[m, c, z] = r
            pb[m, c, z + 1] = roots[m, z + 1] * r
            core = r[0, 0:rows]
            r_core[m, c, z] = core
            acc = acc + core * core
        return acc

    def image_step(m, z, ra, aa):
        for c in range(2):
            r = r_ext[m, c, z]
            a = image(m, c, z, r, pb)
            a_ext[m, c, z] = a
            pa[m, c, z + 1] = roots[m, z + 1] * a
            core = a[0, 0:rows]
            a_core[m, c, z] = core
            ra = ra + r[0, 0:rows] * core
            aa = aa + core * core
        return ra, aa

    def second_step(m, z, ab):
        for c in range(2):
            a = a_ext[m, c, z]
            b = image(m, c, z, a, pa)
            ab = ab + a[0, 0:rows] * b[0, 0:rows]
        return ab

    peer = {"ens": lax.rem(ie + 1, ne)}

    def to_peer(i, src, dst):
        return pltpu.make_async_remote_copy(
            src_ref=src, dst_ref=dst, send_sem=peer_send.at[i], recv_sem=peer_recv.at[i],
            device_id=peer, device_id_type=mesh_id)

    peer_flows = [to_peer(0, w_core, w_peer)]
    for m in range(members):
        peer_flows.append(to_peer(2 * m + 1, r_core.at[m], r_peer.at[m]))
        peer_flows.append(to_peer(2 * m + 2, a_core.at[m], a_peer.at[m]))

    zero_core = jnp.zeros((rows, cols), jnp.float32)
    grams = []
    for m in range(members):
        assemble(m)
        for z in range(layers):
            roots_step(m, z)
        if m == 0:
            peer_flows[0].start()
            for k in range(1, rounds):
                pl.semaphore_wait(relay.at[k - 1], adjacent_count)
                signal_adjacent(relay.at[k])
        rr = ra = aa = ab = zero_core
        for z in range(layers):
            rr = residual_step(m, z, rr)
        for z in range(layers):
            ra, aa = image_step(m, z, ra, aa)
        peer_flows[2 * m + 1].start()
        for z in range(layers):
            ab = second_step(m, z, ab)
        peer_flows[2 * m + 2].start()
        grams.append((rr, ra, aa, ab))

    lane_1 = iota((1, cols), 1)
    mine = jnp.zeros((1, cols), jnp.float32)
    for m in range(members):
        for q, acc in enumerate(grams[m]):
            value = jnp.sum(jnp.sum(acc, axis=0, keepdims=True), axis=1, keepdims=True)
            mine = jnp.where(lane_1 == 4 * m + q, value, mine)
    gram_s[0] = mine

    if rounds > 0:
        pl.semaphore_wait(relay.at[rounds - 1], adjacent_count)

    def gram_copy(d):
        return pltpu.make_async_remote_copy(
            src_ref=gram_s, dst_ref=gram_r.at[pl.ds(d, 1)],
            send_sem=gram_send, recv_sem=gram_recv,
            device_id=group_target(d), device_id_type=pl.DeviceIdType.MESH)

    each_peer(lambda d: gram_copy(d).start())
    everything = pltpu.make_async_remote_copy(
        src_ref=gram_r.at[pl.ds(1, total - 1)], dst_ref=gram_r.at[pl.ds(1, total - 1)],
        send_sem=gram_send, recv_sem=gram_recv,
        device_id=group_target(1), device_id_type=pl.DeviceIdType.MESH)
    everything.wait_recv()

    half = np_ * nq
    own = mine
    if half > 1:
        own = own + jnp.sum(gram_r[1:half], axis=0)
    sums = [own] + [jnp.sum(gram_r[half * e:half * (e + 1)], axis=0) for e in range(1, ne)]
    steps = []
    for e in range(ne):
        for m in range(members):
            g_rr, g_ra, g_aa, g_ab = [
                jnp.sum(jnp.where(lane_1 == 4 * m + q, sums[e], 0.0), axis=1, keepdims=True)
                for q in range(4)
            ]
            first = g_rr / g_ra
            following = g_rr - 2.0 * first * g_ra + first * first * g_aa
            growth = 1.0 + following / g_rr
            curve = (growth * growth * g_ra - 2.0 * growth * first * g_aa
                     + first * first * g_ab)
            second = following / curve
            share = 1.0 / (members * ne)
            steps.append(((first + second * growth) * share, second * first * share))

    for flow in peer_flows:
        flow.wait_recv()
    share = 1.0 / (members * ne)

    def final_step(z, carry):
        for c in range(2):
            value = share * (w_core[c, z] + w_peer[c, z])
            for m in range(members):
                value = value + steps[m][0] * r_core[m, c, z] - steps[m][1] * a_core[m, c, z]
                one, two = steps[members + m]
                value = value + one * r_peer[m, c, z] - two * a_peer[m, c, z]
            out_ref[c, z] = value
        return carry

    lax.fori_loop(0, layers, final_step, 0)

    for chunk in flows:
        for copy, to_ok, from_ok in chunk:
            pl.when(to_ok)(copy.wait_send)
    for flow in peer_flows:
        flow.wait_send()
    everything.wait_send()


def body(sizes, u_prior, friction_rows, friction_table, bed_fixed, ice_mask):
    members, _, layers, rows, cols = u_prior.shape
    levels = friction_table.shape[0]
    total = sizes[0] * sizes[1] * sizes[2]
    ring = rows + 2 * HALO
    chunks, _ = chunk_places(members, layers)
    pairs = sum(chunk[1] for chunk in chunks)
    groups = sum(chunk[3] for chunk in chunks)
    f32 = jnp.float32
    any_space = pl.BlockSpec(memory_space=pl.ANY)
    vmem = lambda *shape: pltpu.VMEM(shape, f32)
    core = (members, 2, layers, rows, cols)
    wide = (2, ring, cols)
    return pl.pallas_call(
        functools.partial(kernel, sizes),
        out_shape=jax.ShapeDtypeStruct((2, layers, rows, cols), f32),
        in_specs=[any_space] * 5,
        out_specs=pl.BlockSpec(memory_space=pltpu.VMEM),
        scratch_shapes=[
            pltpu.SMEM((members,), jnp.int32), vmem(*core), vmem(levels, rows, cols),
            pltpu.VMEM((rows, cols), jnp.int32), pltpu.VMEM((rows, cols), jnp.int32),
            vmem(pairs, 8, cols), vmem(pairs, 8, cols), vmem(groups, rows, cols), vmem(groups, 8, cols),
            vmem(pairs, 8, cols), vmem(pairs, 8, cols), vmem(2, groups, rows, cols),
            vmem(2, 2, groups, 8, cols), vmem(groups, ring, cols),
            vmem(members, 2, layers + 2, *wide), vmem(members, layers + 2, *wide),
            vmem(members, 2, layers, *wide),
            vmem(members, 2, layers + 2, *wide), vmem(members, 2, layers + 2, *wide),
            vmem(members, 2, layers, *wide), vmem(members, 2, layers, *wide),
            vmem(4 + members, *wide),
            vmem(*core), vmem(*core), vmem(*core[1:]),
            vmem(*core), vmem(*core), vmem(*core[1:]),
            vmem(1, 1, cols), vmem(total, 1, cols),
            pltpu.SemaphoreType.REGULAR((max(sizes[0], sizes[1]),)),
            pltpu.SemaphoreType.DMA((5,)),
            pltpu.SemaphoreType.DMA((8 * members,)), pltpu.SemaphoreType.DMA((8 * members,)),
            pltpu.SemaphoreType.DMA((2 * members + 1,)), pltpu.SemaphoreType.DMA((2 * members + 1,)),
            pltpu.SemaphoreType.DMA, pltpu.SemaphoreType.DMA,
        ],
        compiler_params=pltpu.CompilerParams(
            collective_id=0, has_side_effects=True),
        name="picard",
    )(friction_rows, u_prior, friction_table, bed_fixed, ice_mask)


def solution(mesh):
    sizes = (mesh.shape["plane"], mesh.shape["planey"], mesh.shape["ens"])
    in_specs = (
        P(("group", "ens"), None, None, "plane", "planey"),
        P(("group", "ens")),
        P("group", "plane", "planey"),
        P("plane", "planey"),
        P("plane", "planey"),
    )
    out_specs = P("group", None, "plane", "planey")
    return jax.shard_map(functools.partial(body, sizes), mesh=mesh, in_specs=in_specs,
                         out_specs=out_specs, check_vma=False)
```

profile of v0, /device:TPU:0, one launch (start us, length us, event | category | flops | bytes accessed | tf_op | source)
XLA Modules:
  0.0 19.9 jit_solution(15344026692700223578)
XLA Ops:
  0.0 18.2 %picard.1 = f32[2,10,16,128]{3,2,1,0:T(8,128)} custom-call(s32[2]{0:T(128)} %rows_hbm.1, f32[2,2,10,16,128]{4,3,2,1,0:T(8,128)} %u_hbm.1, f32[16,16,128]{2,1,0:T(8,128)} %table_hbm.1, s32[16,128]{1,0:T(8,128)} %bed_hbm.1, s32[16,128]{1,0:T(8,128)} %mask_hbm.1), custom_call_target="tpu_custom_call" | custom-call | tf_op jit(solution)/shard_map/picard/pallas_call | solution.py:423
  18.3 1.6 %copy.7 = f32[2,10,16,128]{3,2,1,0:T(8,128)} copy(f32[2,10,16,128]{3,2,1,0:T(8,128)} %picard.1) | data formatting | bytes 327680
where the time goes:
time: 20 us; the launch traced here: 19.9 us
  Pallas kernels  18.2 us (91%)
  local copies, waits for them, and re-layouts  1.59 us (8%)
    pallas_call x1, Pallas kernels, body(): pl.pallas_call(functools.partial(kernel, sizes), out_shape=jax.ShapeDtype...  18.2 us
    unnamed x1, local copies, waits for them, and re-layouts  1.59 us

commit v1 on v0

--- a/solution.py
+++ b/solution.py
@@ -422,7 +422,7 @@
     wide = (2, ring, cols)
     return pl.pallas_call(
         functools.partial(kernel, sizes),
-        out_shape=jax.ShapeDtypeStruct((2, layers, rows, cols), f32),
+        out_shape=pltpu.VMEM((2, layers, rows, cols), f32),
         in_specs=[any_space] * 5,
         out_specs=pl.BlockSpec(memory_space=pltpu.VMEM),
         scratch_shapes=[
@@ -446,9 +446,10 @@
             pltpu.SemaphoreType.DMA, pltpu.SemaphoreType.DMA,
         ],
         compiler_params=pltpu.CompilerParams(
-            collective_id=0, has_side_effects=True),
+            collective_id=0, has_side_effects=True, vmem_limit_bytes=24 << 20),
         name="picard",
-    )(friction_rows, u_prior, friction_table, bed_fixed, ice_mask)
+    )(*[pltpu.with_memory_space_constraint(x, pltpu.HBM) for x in (
+        friction_rows, u_prior, friction_table, bed_fixed, ice_mask)])
 
 
 def solution(mesh):

time: 20 us -> 18.4 us (0.920)
  local copies, waits for them, and re-layouts: 1.59 us -> 0.67 us
  Pallas kernels: 18.2 us -> 17.6 us
    unnamed x1, local copies, waits for them, and re-layouts: 1.59 us -> 0.67 us
    pallas_call x1, Pallas kernels: 18.2 us -> 17.6 us  [body(): pl.pallas_call(functools.partial(kernel, sizes), out_shape=pltpu.VMEM((2,...]
where the time goes in v1:
time: 18.4 us; the launch traced here: 18.3 us
  Pallas kernels  17.6 us (96%)
  local copies, waits for them, and re-layouts  0.67 us (4%)
    pallas_call x1, Pallas kernels, body(): pl.pallas_call(functools.partial(kernel, sizes), out_shape=pltpu.VMEM((2,...  17.6 us
    unnamed x1, local copies, waits for them, and re-layouts  0.67 us

profile of v1, /device:TPU:0, one launch (start us, length us, event | category | flops | bytes accessed | tf_op | source)
XLA Modules:
  0.0 18.3 jit_solution(521626991165757516)
XLA Ops:
  0.0 17.6 %picard.1 = f32[2,10,16,128]{3,2,1,0:T(8,128)S(1)} custom-call(s32[2]{0:T(128)} %rows_hbm.1, f32[2,2,10,16,128]{4,3,2,1,0:T(8,128)} %u_hbm.1, f32[16,16,128]{2,1,0:T(8,128)} %table_hbm.1, s32[16,128]{1,0:T(8,128)} %bed_hbm.1, s32[16,128]{1,0:T(8,128)} %mask_hbm.1), custom_call_target="tpu_custom_call" | custom-call | tf_op jit(solution)/shard_map/picard/pallas_call | solution.py:423
  17.6 0.7 %copy.7 = f32[2,10,16,128]{3,2,1,0:T(8,128)} copy(f32[2,10,16,128]{3,2,1,0:T(8,128)S(1)} %picard.1) | data formatting | bytes 327680

commit v2 on v1

v2 whole, which is shorter than its diff:
```python
import functools
import math
import numpy as np
import jax
import jax.numpy as jnp
from jax import lax
from jax.experimental import pallas as pl
from jax.experimental.pallas import tpu as pltpu
from jax.sharding import PartitionSpec as P

bed_unit = 2.0 ** (-29)
HALO = 4
TOP = 8
SPAN = 24
TALL = 144
PAD = 160
STEP_I = (0.25, 0.125)
STEP_J = (0.125, 0.25)


def iota(shape, dim):
    return lax.broadcasted_iota(jnp.int32, shape, dim)


def turn(x, step):
    return pltpu.roll(x, step % x.shape[1], 1)


def stencils(layers, members, lanes):
    def matrix(entry):
        out = np.zeros((lanes, lanes), np.float32)
        for z in range(layers):
            for i in range(-HALO, SPAN - HALO):
                for dz in (-1, 0, 1):
                    for di in (-1, 0, 1):
                        if 0 <= z + dz < layers and -HALO <= i + di < SPAN - HALO:
                            out[(z + dz) * SPAN + (i + di) % SPAN, z * SPAN + i % SPAN] = entry(dz, di)
        return out

    def copies(slot, targets, steps):
        out = np.zeros((lanes, lanes), np.float32)
        for z in targets:
            for i in range(-HALO, SPAN - HALO):
                for di, weight in steps:
                    if -HALO <= i + di < SPAN - HALO:
                        out[slot * SPAN + (i + di) % SPAN, z * SPAN + i % SPAN] = weight
        return out

    same, difference = ((0, 1.0),), ((1, 1.0), (-1, -1.0))
    every = range(layers)
    out = [matrix(lambda dz, di, c=c: (2.0 - abs(dz)) * (STEP_I[c] if di else 1.0)) for c in range(2)]
    out.append(matrix(lambda dz, di: 0.0 if dz else float(di)))
    out.append(matrix(lambda dz, di: 0.0 if di else float(dz)))
    out += [copies(1, every, same), copies(0, every, same), copies(0, every, difference)]
    out += [copies(2 + m, (0,), same) for m in range(members)]
    return np.stack(out)


def kernel(sizes, rows_hbm, u_hbm, table_hbm, bed_hbm, mask_hbm, matrix_hbm, out_ref,
           rows_ref, flat, table_v, bed_v, mask_v, matrix,
           up_s, down_s, side_s, corner_s,
           below_r, above_r, side_r, corner_r,
           tall, cover, roots, tr, pa, pb, r_ext, a_ext, force,
           w_core, r_core, a_core, r_peer, a_peer, w_peer, gram_s, gram_r, blank, wide_blank,
           relay, in_sem, halo_send, halo_recv, peer_send, peer_recv, gram_send, gram_recv):
    np_, nq, ne = sizes
    members, _, layers, rows, cols = u_hbm.shape
    ix, iy, ie = lax.axis_index("plane"), lax.axis_index("planey"), lax.axis_index("ens")
    total = np_ * nq * ne
    mesh_id = pl.DeviceIdType.MESH
    fixed = 2 + members
    lanes = 2 * cols
    assert rows + 2 * HALO == SPAN and cols == 128 and layers * SPAN <= lanes and fixed <= layers
    other = 2 * members

    loads = [
        pltpu.make_async_copy(src, dst, in_sem.at[i])
        for i, (src, dst) in enumerate(
            [(u_hbm.at[m], flat.at[pl.ds(2 * m, 2), pl.ds(0, layers), pl.ds(0, rows)])
             for m in range(members)]
            + [(table_hbm, table_v), (bed_hbm, bed_v), (mask_hbm, mask_v), (rows_hbm, rows_ref),
               (matrix_hbm, matrix)])
    ]
    for load in loads:
        load.start()
    late = loads.pop()

    adjacent = []
    for dx in (0, -1, 1):
        for dy in (0, -1, 1):
            for de in range(ne):
                if (dx, dy, de) == (0, 0, 0):
                    continue
                tx, ty = ix + dx, iy + dy
                ok = (tx >= 0) & (tx < np_) & (ty >= 0) & (ty < nq)
                where = {"plane": jnp.clip(tx, 0, np_ - 1), "planey": jnp.clip(ty, 0, nq - 1),
                         "ens": lax.rem(ie + de, ne)}
                adjacent.append((ok, where))
    span_x = 1 + (ix > 0).astype(jnp.int32) + (ix < np_ - 1).astype(jnp.int32)
    span_y = 1 + (iy > 0).astype(jnp.int32) + (iy < nq - 1).astype(jnp.int32)
    adjacent_count = span_x * span_y * ne - 1
    rounds = max(max(np_, nq) - 2, 0)

    def signal_adjacent(sem):
        for ok, where in adjacent:
            @pl.when(ok)
            def _(where=where):
                pl.semaphore_signal(sem, inc=1, device_id=where, device_id_type=mesh_id)

    barrier = pltpu.get_barrier_semaphore()
    signal_adjacent(barrier)

    def group_target(d):
        de, rest = d // (np_ * nq), d % (np_ * nq)
        return {
            "plane": lax.rem(ix + rest // nq, np_),
            "planey": lax.rem(iy + rest % nq, nq),
            "ens": lax.rem(ie + de, ne),
        }

    def each_peer(fn):
        if total <= 32:
            for d in range(1, total):
                fn(d)
        else:
            def step(d, carry):
                fn(d)
                return carry
            lax.fori_loop(1, total, step, 0)

    planes = [
        ([(other, k) for k in range(fixed + fixed % 2)] if m == 0 else [])
        + [(2 * m + c, z) for z in range(layers) for c in range(2)]
        for m in range(members)
    ]
    pair_at = [sum(len(p) for p in planes[:m]) // 2 for m in range(members)]
    pair_count = [len(p) // 2 for p in planes]
    side_tiles = [((2 * m, 2 * m + 1), m) for m in range(members)] + [((other,), 0)]
    tile_at = [[t for t, (_, k) in enumerate(side_tiles) if k == m] for m in range(members)]

    has_up, has_down = ix > 0, ix < np_ - 1
    has_left, has_right = iy > 0, iy < nq - 1
    rims, flanks = [[] for _ in planes], [[] for _ in planes]
    absent = []
    for dx, dy, src, dst in (
        (-1, -1, corner_s.at[0, 0], corner_r.at[1, 1]),
        (-1, 1, corner_s.at[0, 1], corner_r.at[1, 0]),
        (1, -1, corner_s.at[1, 0], corner_r.at[0, 1]),
        (1, 1, corner_s.at[1, 1], corner_r.at[0, 0]),
        (0, -1, side_s.at[0], side_r.at[1]),
        (0, 1, side_s.at[1], side_r.at[0]),
        (-1, 0, up_s, below_r),
        (1, 0, down_s, above_r),
    ):
        tx, ty = ix + dx, iy + dy
        sx, sy = ix - dx, iy - dy
        to_ok = (tx >= 0) & (tx < np_) & (ty >= 0) & (ty < nq)
        from_ok = (sx >= 0) & (sx < np_) & (sy >= 0) & (sy < nq)
        absent.append((jnp.logical_not(from_ok), dst))
        for k in range(members):
            if dy:
                parts = [pl.ds(t, 1) for t in tile_at[k]]
            elif k == 0:
                head = pair_count[0] // 2
                parts = [pl.ds(0, head), pl.ds(head, pair_count[0] - head)]
            else:
                parts = [pl.ds(pair_at[k], pair_count[k])]
            for part in parts:
                copy = pltpu.make_async_remote_copy(
                    src_ref=src.at[part], dst_ref=dst.at[part],
                    send_sem=halo_send, recv_sem=halo_recv.at[k],
                    device_id={"plane": jnp.clip(tx, 0, np_ - 1), "planey": jnp.clip(ty, 0, nq - 1)},
                    device_id_type=mesh_id)
                (flanks if dy else rims)[k].append((to_ok, copy))

    def tiles(count):
        return blank.at[pl.ds(0, count)]

    def settle(chunk_list, received):
        for up in (0, 1):
            for down in (0, 1):
                for left in (0, 1):
                    for right in (0, 1):
                        if (up + down > np_ - 1 or left + right > nq - 1
                                or (np_ > 1 and up + down == 0) or (nq > 1 and left + right == 0)):
                            continue
                        count = sum(
                            pair_count[k] * (up + down)
                            + len(tile_at[k]) * (2 + up + down) * (left + right) for k in chunk_list)
                        if count == 0:
                            continue
                        here = ((has_up == bool(up)) & (has_down == bool(down))
                                & (has_left == bool(left)) & (has_right == bool(right)))
                        bulk = pltpu.make_async_remote_copy(
                            src_ref=tiles(count), dst_ref=tiles(count), send_sem=halo_send,
                            recv_sem=halo_recv.at[chunk_list[0]],
                            device_id={"ens": lax.rem(ie + 1, ne)}, device_id_type=mesh_id)
                        pl.when(here)(bulk.wait_recv if received else bulk.wait_send)

    rim = jnp.zeros((SPAN - rows, cols), jnp.float32)
    for f in range(other + 1):
        flat[f, layers] = jnp.zeros((SPAN, cols), jnp.float32)
        for z in range(layers):
            flat[f, z, pl.ds(rows, SPAN - rows)] = rim
    for k in range(fixed, layers):
        flat[other, k, pl.ds(0, rows)] = jnp.zeros((rows, cols), jnp.float32)

    for load in loads:
        load.wait()

    cover_core = mask_v[...].astype(jnp.float32)
    flat[other, 0, pl.ds(0, rows)] = bed_v[...].astype(jnp.float32) * bed_unit
    flat[other, 1, pl.ds(0, rows)] = cover_core
    for m in range(members):
        flat[other, 2 + m, pl.ds(0, rows)] = table_v[rows_ref[m]]
    for m in range(members):
        for i, at in enumerate(planes[m]):
            half = pl.ds(HALO * (i % 2), HALO)
            up_s[pair_at[m] + i // 2, half] = flat[at + (pl.ds(0, HALO),)]
            down_s[pair_at[m] + i // 2, half] = flat[at + (pl.ds(rows - HALO, HALO),)]

    pl.semaphore_wait(barrier, adjacent_count)

    def send(chosen):
        for to_ok, copy in chosen:
            pl.when(to_ok)(copy.start)

    send(rims[0][0::2])

    lane8 = iota((8, cols), 1)

    def places(start, offset):
        out = None
        for z in range(layers):
            low = z * SPAN + start - offset
            if -HALO < low < cols:
                here = (lane8 >= low) & (lane8 < low + HALO)
                out = here if out is None else out | here
        return out

    def stood_up(f):
        plain = flat[f].reshape((layers + 1) * SPAN, cols)
        return [plain[cols * h:cols * (h + 1)].T for h in range(2)]

    for fields, k in side_tiles:
        edges = []
        for f in fields:
            halves = stood_up(f)
            edges.append([[half[start:start + HALO] for half in halves] for start in (0, cols - HALO)])
        if len(edges) == 1:
            edges.append([[jnp.zeros((HALO, cols), jnp.float32)] * 2] * 2)
        t = side_tiles.index((fields, k))
        for h in range(2):
            pair = [jnp.concatenate([edges[0][h][q], edges[1][h][q]], axis=0) for q in range(2)]
            side_s[h, t, 0] = pair[0]
            side_s[h, t, 1] = pair[1]
            corner_s[0, h, t] = jnp.where(places(0, 0), pair[0], pair[1])
            corner_s[1, h, t] = jnp.where(places(rows - HALO, 0), pair[0], pair[1])
    send(flanks[0])
    send(rims[0][1::2])
    for k in range(1, members):
        send(flanks[k])
        send(rims[k])
    if rounds > 0:
        signal_adjacent(relay.at[0])

    for gone, dst in absent:
        @pl.when(gone)
        def _(dst=dst):
            dst[...] = jnp.zeros(dst.shape, jnp.float32)
    for c in range(2):
        for z in range(layers):
            summed = flat[c, z, pl.ds(0, rows)]
            for m in range(1, members):
                summed = summed + flat[2 * m + c, z, pl.ds(0, rows)]
            w_core[c, z] = cover_core * summed

    peer = {"ens": lax.rem(ie + 1, ne)}

    def to_peer(src, dst):
        return pltpu.make_async_remote_copy(
            src_ref=src, dst_ref=dst, send_sem=peer_send, recv_sem=peer_recv,
            device_id=peer, device_id_type=mesh_id)

    send_w = to_peer(w_core, w_peer)
    send_r = [to_peer(r_core.at[m], r_peer.at[m]) for m in range(members)]
    send_a = [to_peer(a_core.at[m], a_peer.at[m]) for m in range(members)]
    send_w.start()

    def relay_on(k):
        pl.semaphore_wait(relay.at[k - 1], adjacent_count)
        signal_adjacent(relay.at[k])

    if rounds > 1:
        relay_on(1)
    late.wait()

    def at(ref, index, base, count=TALL):
        return ref[index + (pl.ds(base, count),)]

    def assemble(k):
        settle([k], True)
        for i, place in enumerate(planes[k]):
            half = pl.ds(HALO * (i % 2), HALO)
            pair = pair_at[k] + i // 2
            flat[place + (pl.ds(rows, HALO),)] = below_r[pair, half]
            flat[place + (pl.ds(rows + HALO, HALO),)] = above_r[pair, half]
        for t in tile_at[k]:
            for h in range(2):
                over = turn(corner_r[0, h, t], SPAN - rows)
                under = turn(corner_r[1, h, t], rows)
                whole = []
                for q in range(2):
                    part = jnp.where(places(rows + HALO, cols * q), over, side_r[h, t, q])
                    whole.append(jnp.where(places(rows, cols * q), under, part))
                start = TOP + cols if h else TOP - HALO
                for n, f in enumerate(side_tiles[t][0]):
                    for q in range(2):
                        tall[f, pl.ds(start, HALO), pl.ds(cols * q, cols)] = (
                            whole[q][HALO * n:HALO * (n + 1)])
            for f in side_tiles[t][0]:
                for q, half in enumerate(stood_up(f)):
                    tall[f, pl.ds(TOP, cols), pl.ds(cols * q, cols)] = half

    def split(x):
        high = x.astype(jnp.bfloat16)
        return [high, (x - high.astype(jnp.float32)).astype(jnp.bfloat16)]

    def times(k, *values):
        n = values[0].shape[0]
        out = jnp.dot(jnp.concatenate(sum([split(x) for x in values], []), axis=0), matrix[k],
                      preferred_element_type=jnp.float32)
        return [out[2 * n * i:2 * n * i + n] + out[2 * n * i + n:2 * n * i + 2 * n]
                for i in range(len(values))]

    root_base, res_base, img_base = TOP - 3, TOP - 2, TOP - 1
    lane = iota((8, lanes), 1)
    layer = sum([(lane >= SPAN * z).astype(jnp.int32) for z in range(1, layers + 1)])
    place = lane - SPAN * layer
    inside = ((place < rows) & (layer < layers)).astype(jnp.float32)[0:1]

    def prepare():
        b = res_base
        cover[pl.ds(root_base, TALL)] = jnp.dot(
            at(tall, (other,), root_base).astype(jnp.bfloat16), matrix[4],
            preferred_element_type=jnp.float32)

    def prepare_force():
        b = res_base
        row = (ix * rows + jnp.where(place < rows + HALO, place, place - SPAN))[0:1]
        thickness = 1.0 + 2.0 * row.astype(jnp.float32) / (np_ * rows - 1)
        covered = at(cover, (), b)
        field = at(tall, (other,), b)
        (slope_x,) = times(6, field)
        (slope_y,) = times(5, at(tall, (other,), b + 1) - at(tall, (other,), b - 1))
        force[0] = -(covered * thickness * (slope_x * 0.5))
        force[1] = -(covered * thickness * (slope_y * 0.5))
        for m in range(members):
            (friction,) = times(7 + m, field)
            force[2 + m] = (1.0 - covered) + covered * friction

    def roots_level(m):
        b = root_base
        u, v = at(tall, (2 * m,), b), at(tall, (2 * m + 1,), b)
        u_i, v_i = times(2, u, v)
        u_z, v_z = times(3, u, v)
        u_j = at(tall, (2 * m,), b + 1) - at(tall, (2 * m,), b - 1)
        v_j = at(tall, (2 * m + 1,), b + 1) - at(tall, (2 * m + 1,), b - 1)
        shear = u_j + v_i
        strain = (4.0 * (u_i * (u_i + v_j) + v_j * v_j) + shear * shear
                  + (u_z * u_z + v_z * v_z)) * 0.0625
        root = at(cover, (), b) * (
            math.sqrt(2.0) * jnp.exp(jnp.log(strain + 0.1) * (-1.0 / 6.0)))
        roots[m, pl.ds(b, TALL)] = root
        pa[m, 0, pl.ds(b, TALL)] = root * u
        pa[m, 1, pl.ds(b, TALL)] = root * v

    def lean(ref, index, base, c):
        return at(ref, index, base) + STEP_J[c] * (at(ref, index, base - 1) + at(ref, index, base + 1))

    def residual_level(m):
        b = res_base
        for c in range(2):
            near, moved = times(c, lean(roots, (m,), b, c), lean(pa, (m, c), b, c))
            root = at(roots, (m,), b)
            weight = root * near + force[2 + m]
            r = force[c] - (weight * (at(cover, (), b) * at(tall, (2 * m + c,), b)) - root * moved)
            tr[m, c, pl.ds(b, TALL)] = weight
            r_ext[m, c, pl.ds(b, TALL)] = r
            pb[m, c, pl.ds(b, TALL)] = root * r

    def image_level(m):
        b = img_base
        for c in range(2):
            (moved,) = times(c, lean(pb, (m, c), b, c))
            root = at(roots, (m,), b)
            a = at(tr, (m, c), b) * at(r_ext, (m, c), b) - root * moved
            a_ext[m, c, pl.ds(b, TALL)] = a
            pa[m, c, pl.ds(b, TALL)] = root * a

    def second_level(m):
        def fold(x):
            out = x[0:8]
            for start in range(8, cols, 8):
                out = out + x[start:start + 8]
            return out

        sums = [None] * 4
        for c in range(2):
            scaled = at(pa, (m, c), TOP, cols)
            (out,) = times(c, scaled + (2.0 * STEP_J[c]) * at(pa, (m, c), TOP - 1, cols))
            r, a = at(r_ext, (m, c), TOP, cols), at(a_ext, (m, c), TOP, cols)
            square = a * a
            terms = [fold(x) for x in (r * r, r * a, square,
                                       at(tr, (m, c), TOP, cols) * square - scaled * out)]
            sums = terms if c == 0 else [s + t for s, t in zip(sums, terms)]
        return [inside * jnp.sum(s, axis=0, keepdims=True) for s in sums]

    grams = []
    for m in range(members):
        assemble(m)
        if m == 0:
            prepare()
        roots_level(m)
        if m == 0:
            prepare_force()
        if m > 0:
            image_level(m - 1)
        residual_level(m)
        if m > 0:
            grams.append(second_level(m - 1))
        if m == 0:
            for k in range(2, rounds):
                relay_on(k)
    image_level(members - 1)
    grams.append(second_level(members - 1))

    lane_1 = iota((1, cols), 1)
    mine = jnp.zeros((1, cols), jnp.float32)
    for m in range(members):
        for q, acc in enumerate(grams[m]):
            mine = jnp.where(lane_1 == 4 * m + q, jnp.sum(acc, axis=1, keepdims=True), mine)
    gram_s[0] = mine

    if rounds > 0:
        pl.semaphore_wait(relay.at[rounds - 1], adjacent_count)

    def gram_copy(d):
        return pltpu.make_async_remote_copy(
            src_ref=gram_s, dst_ref=gram_r.at[pl.ds(d, 1)],
            send_sem=gram_send, recv_sem=gram_recv,
            device_id=group_target(d), device_id_type=pl.DeviceIdType.MESH)

    each_peer(lambda d: gram_copy(d).start())

    def lie_down(src, dst):
        for c in range(2):
            whole = src[c, pl.ds(TOP, cols)]
            flat_rows = jnp.concatenate(
                [whole[:, cols * q:cols * (q + 1)].T for q in range(2)], axis=0)
            for z in range(layers):
                dst[c, z] = flat_rows[SPAN * z:SPAN * z + rows]

    for m in range(members):
        lie_down(r_ext.at[m], r_core.at[m])
        send_r[m].start()
        lie_down(a_ext.at[m], a_core.at[m])
        send_a[m].start()
    everything = pltpu.make_async_remote_copy(
        src_ref=gram_r.at[pl.ds(1, total - 1)], dst_ref=gram_r.at[pl.ds(1, total - 1)],
        send_sem=gram_send, recv_sem=gram_recv,
        device_id=group_target(1), device_id_type=pl.DeviceIdType.MESH)
    everything.wait_recv()

    half = np_ * nq
    own = mine
    if half > 1:
        own = own + jnp.sum(gram_r[1:half], axis=0)
    sums = [own] + [jnp.sum(gram_r[half * e:half * (e + 1)], axis=0) for e in range(1, ne)]
    steps = []
    for e in range(ne):
        for m in range(members):
            g_rr, g_ra, g_aa, g_ab = [
                jnp.sum(jnp.where(lane_1 == 4 * m + q, sums[e], 0.0), axis=1, keepdims=True)
                for q in range(4)
            ]
            first_step = g_rr / g_ra
            following = g_rr - 2.0 * first_step * g_ra + first_step * first_step * g_aa
            growth = 1.0 + following / g_rr
            curve = (growth * growth * g_ra - 2.0 * growth * first_step * g_aa
                     + first_step * first_step * g_ab)
            second_step = following / curve
            share = 1.0 / (members * ne)
            steps.append(((first_step + second_step * growth) * share,
                          second_step * first_step * share))

    peer_part = wide_blank.at[pl.ds(0, 1 + 2 * members)]
    peer_bulk = to_peer(peer_part, peer_part)
    peer_bulk.wait_recv()
    share = 1.0 / (members * ne)

    def final_step(z, carry):
        for c in range(2):
            value = share * (w_core[c, z] + w_peer[c, z])
            for m in range(members):
                one, two = steps[m]
                value = value + one * r_core[m, c, z] - two * a_core[m, c, z]
                one, two = steps[members + m]
                value = value + one * r_peer[m, c, z] - two * a_peer[m, c, z]
            out_ref[c, z] = value
        return carry

    lax.fori_loop(0, layers, final_step, 0)

    settle(list(range(members)), False)
    peer_bulk.wait_send()
    everything.wait_send()


def body(sizes, u_prior, friction_rows, friction_table, bed_fixed, ice_mask):
    members, _, layers, rows, cols = u_prior.shape
    levels = friction_table.shape[0]
    total = sizes[0] * sizes[1] * sizes[2]
    fixed = 2 + members
    pairs = (fixed + fixed % 2 + members * 2 * layers) // 2
    fields, lanes = 2 * members + 1, 2 * cols
    rounds = max(max(sizes[0], sizes[1]) - 2, 1)
    f32 = jnp.float32
    matrices = jnp.asarray(stencils(layers, members, lanes), jnp.bfloat16)
    any_space = pl.BlockSpec(memory_space=pl.ANY)
    vmem = lambda *shape: pltpu.VMEM(shape, f32)
    core = (members, 2, layers, rows, cols)
    tall = (PAD, lanes)
    each = (members, 2) + tall
    inputs = (friction_rows, u_prior, friction_table, bed_fixed, ice_mask, matrices)
    return pl.pallas_call(
        functools.partial(kernel, sizes),
        out_shape=pltpu.VMEM((2, layers, rows, cols), f32),
        in_specs=[any_space] * 6,
        out_specs=pl.BlockSpec(memory_space=pltpu.VMEM),
        scratch_shapes=[
            pltpu.SMEM((members,), jnp.int32), vmem(fields, layers + 1, SPAN, cols),
            vmem(levels, rows, cols),
            pltpu.VMEM((rows, cols), jnp.int32), pltpu.VMEM((rows, cols), jnp.int32),
            pltpu.VMEM(matrices.shape, jnp.bfloat16),
            vmem(pairs, 8, cols), vmem(pairs, 8, cols),
            vmem(2, members + 1, 2, 8, cols), vmem(2, 2, members + 1, 8, cols),
            vmem(pairs, 8, cols), vmem(pairs, 8, cols),
            vmem(2, members + 1, 2, 8, cols), vmem(2, 2, members + 1, 8, cols),
            vmem(fields, *tall), vmem(*tall), vmem(members, *tall),
            vmem(*each), vmem(*each), vmem(*each), vmem(*each), vmem(*each),
            vmem(2 + members, TALL, lanes),
            vmem(*core[1:]), vmem(*core), vmem(*core), vmem(*core), vmem(*core), vmem(*core[1:]),
            vmem(1, 1, cols), vmem(total, 1, cols), vmem(2 * pairs + 8 * (members + 1), 8, cols),
            vmem(1 + 2 * members, *core[1:]),
            pltpu.SemaphoreType.REGULAR((rounds,)),
            pltpu.SemaphoreType.DMA((members + 5,)),
            pltpu.SemaphoreType.DMA, pltpu.SemaphoreType.DMA((members,)),
            pltpu.SemaphoreType.DMA, pltpu.SemaphoreType.DMA,
            pltpu.SemaphoreType.DMA, pltpu.SemaphoreType.DMA,
        ],
        compiler_params=pltpu.CompilerParams(
            collective_id=0, has_side_effects=True, vmem_limit_bytes=40 << 20),
        name="picard",
    )(*[pltpu.with_memory_space_constraint(x, pltpu.HBM) for x in inputs])


def solution(mesh):
    sizes = (mesh.shape["plane"], mesh.shape["planey"], mesh.shape["ens"])
    in_specs = (
        P(("group", "ens"), None, None, "plane", "planey"),
        P(("group", "ens")),
        P("group", "plane", "planey"),
        P("plane", "planey"),
        P("plane", "planey"),
    )
    out_specs = P("group", None, "plane", "planey")
    return jax.shard_map(functools.partial(body, sizes), mesh=mesh, in_specs=in_specs,
                         out_specs=out_specs, check_vma=False)
```

time: 18.4 us -> 17.1 us (0.929)
  Pallas kernels: 17.6 us -> 16.3 us
    pallas_call x1, Pallas kernels: 17.6 us -> 16.3 us  [body(): pl.pallas_call(functools.partial(kernel, sizes), out_shape=pltpu.VMEM((2,...]
where the time goes in v2:
time: 17.1 us; the launch traced here: 17 us
  Pallas kernels  16.3 us (95%)
  local copies, waits for them, and re-layouts  0.67 us (4%)
    pallas_call x1, Pallas kernels, body(): pl.pallas_call(functools.partial(kernel, sizes), out_shape=pltpu.VMEM((2,...  16.3 us
    unnamed x1, local copies, waits for them, and re-layouts  0.67 us

profile of v2, /device:TPU:0, one launch (start us, length us, event | category | flops | bytes accessed | tf_op | source)
XLA Modules:
  0.0 17.0 jit_solution(5128412628768570311)
XLA Ops:
  0.0 16.3 %picard.1 = f32[2,10,16,128]{3,2,1,0:T(8,128)S(1)} custom-call(s32[2]{0:T(128)} %rows_hbm.1, f32[2,2,10,16,128]{4,3,2,1,0:T(8,128)} %u_hbm.1, f32[16,16,128]{2,1,0:T(8,128)} %table_hbm.1, s32[16,128]{1,0:T(8,128)} %bed_hbm.1, s32[16,128]{1,0:T(8,128)} %mask_hbm.1, bf16[9,256,256]{2,1,0:T(8,128)(2,1)} %constant.2.clone.matrix_hbm), custom_call_target="tpu_custom_call" | custom-call | tf_op jit(solution)/shard_map/picard/pallas_call | solution.py:536
  16.3 0.7 %copy.8 = f32[2,10,16,128]{3,2,1,0:T(8,128)} copy(f32[2,10,16,128]{3,2,1,0:T(8,128)S(1)} %picard.1) | data formatting | bytes 327680

commit v3 on v2

v3 whole, which is shorter than its diff:
```python
import functools
import math
import numpy as np
import jax
import jax.numpy as jnp
from jax import lax
from jax.experimental import pallas as pl
from jax.experimental.pallas import tpu as pltpu
from jax.sharding import PartitionSpec as P

bed_unit = 2.0 ** (-29)
HALO = 4
TOP = 8
SPAN = 24
TALL = 144
PAD = 160
STEP = 16
STEP_I = (0.25, 0.125)
STEP_J = (0.125, 0.25)


def iota(shape, dim):
    return lax.broadcasted_iota(jnp.int32, shape, dim)


def turn(x, step):
    return pltpu.roll(x, step % x.shape[1], 1)


def stencils(layers, members, lanes):
    def matrix(entry):
        out = np.zeros((lanes, lanes), np.float32)
        for z in range(layers):
            for i in range(-HALO, SPAN - HALO):
                for dz in (-1, 0, 1):
                    for di in (-1, 0, 1):
                        if 0 <= z + dz < layers and -HALO <= i + di < SPAN - HALO:
                            out[(z + dz) * SPAN + (i + di) % SPAN, z * SPAN + i % SPAN] = entry(dz, di)
        return out

    def copies(slot, targets, steps):
        out = np.zeros((lanes, lanes), np.float32)
        for z in targets:
            for i in range(-HALO, SPAN - HALO):
                for di, weight in steps:
                    if -HALO <= i + di < SPAN - HALO:
                        out[slot * SPAN + (i + di) % SPAN, z * SPAN + i % SPAN] = weight
        return out

    same, difference = ((0, 1.0),), ((1, 1.0), (-1, -1.0))
    every = range(layers)
    out = [matrix(lambda dz, di, c=c: (2.0 - abs(dz)) * (STEP_I[c] if di else 1.0)) for c in range(2)]
    out.append(matrix(lambda dz, di: 0.0 if dz else float(di)))
    out.append(matrix(lambda dz, di: 0.0 if di else float(dz)))
    out += [copies(1, every, same), copies(0, every, same), copies(0, every, difference)]
    out += [copies(2 + m, (0,), same) for m in range(members)]
    return np.stack(out)


def kernel(sizes, rows_hbm, u_hbm, table_hbm, bed_hbm, mask_hbm, matrix_hbm, out_ref,
           rows_ref, flat, table_v, bed_v, mask_v, matrix,
           up_s, down_s, side_s, corner_s,
           below_r, above_r, side_r, corner_r,
           tall, cover, roots, tr, pa, pb, r_ext, a_ext, force,
           w_core, r_core, a_core, r_peer, a_peer, w_peer, gram_s, gram_r, gram_blank, blank, wide_blank,
           relay, in_sem, halo_send, halo_recv, peer_send, peer_recv, gram_send, gram_recv):
    np_, nq, ne = sizes
    members, _, layers, rows, cols = u_hbm.shape
    ix, iy, ie = lax.axis_index("plane"), lax.axis_index("planey"), lax.axis_index("ens")
    total = np_ * nq * ne
    mesh_id = pl.DeviceIdType.MESH
    fixed = 2 + members
    lanes = 2 * cols
    assert rows + 2 * HALO == SPAN and cols == 128 and layers * SPAN <= lanes and fixed <= layers
    other = 2 * members

    reach = max(np_, nq)
    rounds = reach - 2 if reach > 3 else reach - 1

    def neighbours(every_core):
        found = []
        for dx, dy in ((-1, -1), (-1, 1), (1, -1), (1, 1), (-1, 0), (1, 0), (0, -1), (0, 1), (0, 0)):
            for de in range(ne):
                if (dx, dy, de) == (0, 0, 0) or (de and (dx or dy) and not every_core):
                    continue
                tx, ty = ix + dx, iy + dy
                ok = (tx >= 0) & (tx < np_) & (ty >= 0) & (ty < nq)
                where = {"plane": jnp.clip(tx, 0, np_ - 1), "planey": jnp.clip(ty, 0, nq - 1),
                         "ens": lax.rem(ie + de, ne)}
                found.append((ok if dx or dy else None, where))
        return found

    span_x = 1 + (ix > 0).astype(jnp.int32) + (ix < np_ - 1).astype(jnp.int32)
    span_y = 1 + (iy > 0).astype(jnp.int32) + (iy < nq - 1).astype(jnp.int32)
    near_count = span_x * span_y + ne - 2
    wide_count = span_x * span_y * ne - 1

    def signal(sem, every_core):
        for ok, where in neighbours(every_core):
            def tell(where=where):
                pl.semaphore_signal(sem, inc=1, device_id=where, device_id_type=mesh_id)
            tell() if ok is None else pl.when(ok)(tell)

    barrier = pltpu.get_barrier_semaphore()
    signal(barrier, False)

    loads = [
        pltpu.make_async_copy(src, dst, in_sem.at[i])
        for i, (src, dst) in enumerate(
            [(u_hbm.at[m], flat.at[pl.ds(2 * m, 2), pl.ds(0, layers), pl.ds(0, rows)])
             for m in range(members)]
            + [(table_hbm, table_v), (bed_hbm, bed_v), (mask_hbm, mask_v), (rows_hbm, rows_ref),
               (matrix_hbm, matrix)])
    ]
    for load in loads:
        load.start()
    late = loads.pop()

    def group_place(d):
        de, rest = d // (np_ * nq), d % (np_ * nq)
        return (lax.rem(2 * np_ - 1 - ix + rest // nq, np_), lax.rem(2 * nq - 1 - iy + rest % nq, nq),
                lax.rem(ie + de, ne))

    def each_peer(fn):
        if total <= 32:
            for d in range(total):
                fn(d)
        else:
            def step(d, carry):
                fn(d)
                return carry
            lax.fori_loop(0, total, step, 0)

    planes = [[(other, k) for k in range(fixed + fixed % 2)]] + [
        [(2 * m + c, z) for z in range(layers) for c in range(2)] for m in range(members)]
    fields = [(other,)] + [(2 * m, 2 * m + 1) for m in range(members)]
    chunks = range(len(planes))
    pair_at = [sum(len(p) for p in planes[:k]) // 2 for k in chunks]
    pair_count = [len(p) // 2 for p in planes]

    has_up, has_down = ix > 0, ix < np_ - 1
    has_left, has_right = iy > 0, iy < nq - 1
    flows = [[] for _ in chunks]
    absent = []
    for dx, dy, src, dst in (
        (-1, -1, corner_s.at[0, 0], corner_r.at[1, 1]),
        (-1, 1, corner_s.at[0, 1], corner_r.at[1, 0]),
        (1, -1, corner_s.at[1, 0], corner_r.at[0, 1]),
        (1, 1, corner_s.at[1, 1], corner_r.at[0, 0]),
        (0, -1, side_s.at[0], side_r.at[1]),
        (0, 1, side_s.at[1], side_r.at[0]),
        (-1, 0, up_s, below_r),
        (1, 0, down_s, above_r),
    ):
        tx, ty = ix + dx, iy + dy
        sx, sy = ix - dx, iy - dy
        to_ok = (tx >= 0) & (tx < np_) & (ty >= 0) & (ty < nq)
        from_ok = (sx >= 0) & (sx < np_) & (sy >= 0) & (sy < nq)
        absent.append((jnp.logical_not(from_ok), dst))
        for k in chunks:
            part = pl.ds(k, 1) if dy else pl.ds(pair_at[k], pair_count[k])
            copy = pltpu.make_async_remote_copy(
                src_ref=src.at[part], dst_ref=dst.at[part],
                send_sem=halo_send, recv_sem=halo_recv.at[k],
                device_id={"plane": jnp.clip(tx, 0, np_ - 1), "planey": jnp.clip(ty, 0, nq - 1)},
                device_id_type=mesh_id)
            flows[k].append((to_ok, copy))

    def tiles(count):
        return blank.at[pl.ds(0, count)]

    def settle(chunk_list, received):
        for up in (0, 1):
            for down in (0, 1):
                for left in (0, 1):
                    for right in (0, 1):
                        if (up + down > np_ - 1 or left + right > nq - 1
                                or (np_ > 1 and up + down == 0) or (nq > 1 and left + right == 0)):
                            continue
                        count = sum(
                            pair_count[k] * (up + down) + (2 + up + down) * (left + right)
                            for k in chunk_list)
                        if count == 0:
                            continue
                        here = ((has_up == bool(up)) & (has_down == bool(down))
                                & (has_left == bool(left)) & (has_right == bool(right)))
                        bulk = pltpu.make_async_remote_copy(
                            src_ref=tiles(count), dst_ref=tiles(count), send_sem=halo_send,
                            recv_sem=halo_recv.at[chunk_list[0]],
                            device_id={"ens": lax.rem(ie + 1, ne)}, device_id_type=mesh_id)
                        pl.when(here)(bulk.wait_recv if received else bulk.wait_send)

    rim = jnp.zeros((SPAN - rows, cols), jnp.float32)
    for f in range(other + 1):
        flat[f, layers] = jnp.zeros((SPAN, cols), jnp.float32)
        for z in range(layers):
            flat[f, z, pl.ds(rows, SPAN - rows)] = rim
    for k in range(fixed, layers):
        flat[other, k, pl.ds(0, rows)] = jnp.zeros((rows, cols), jnp.float32)

    for load in loads:
        load.wait()

    cover_core = mask_v[...].astype(jnp.float32)
    flat[other, 0, pl.ds(0, rows)] = bed_v[...].astype(jnp.float32) * bed_unit
    flat[other, 1, pl.ds(0, rows)] = cover_core
    for m in range(members):
        flat[other, 2 + m, pl.ds(0, rows)] = table_v[rows_ref[m]]
    lane8 = iota((8, cols), 1)

    def places(start, offset):
        out = None
        for z in range(layers):
            low = z * SPAN + start - offset
            if -HALO < low < cols:
                here = (lane8 >= low) & (lane8 < low + HALO)
                out = here if out is None else out | here
        return out

    def stood_up(f):
        plain = flat[f].reshape((layers + 1) * SPAN, cols)
        return [plain[cols * h:cols * (h + 1)].T for h in range(2)]

    for k in chunks:
        for i, at in enumerate(planes[k]):
            half = pl.ds(HALO * (i % 2), HALO)
            up_s[pair_at[k] + i // 2, half] = flat[at + (pl.ds(0, HALO),)]
            down_s[pair_at[k] + i // 2, half] = flat[at + (pl.ds(rows - HALO, HALO),)]
        edges = []
        for f in fields[k]:
            halves = stood_up(f)
            edges.append([[half[start:start + HALO] for half in halves] for start in (0, cols - HALO)])
        if len(edges) == 1:
            edges.append([[jnp.zeros((HALO, cols), jnp.float32)] * 2] * 2)
        for h in range(2):
            pair = [jnp.concatenate([edges[0][h][q], edges[1][h][q]], axis=0) for q in range(2)]
            side_s[h, k, 0] = pair[0]
            side_s[h, k, 1] = pair[1]
            corner_s[0, h, k] = jnp.where(places(0, 0), pair[0], pair[1])
            corner_s[1, h, k] = jnp.where(places(rows - HALO, 0), pair[0], pair[1])

    pl.semaphore_wait(barrier, near_count)
    for chunk in flows:
        for to_ok, copy in chunk:
            pl.when(to_ok)(copy.start)
    if rounds > 0:
        signal(relay.at[0], False)

    for gone, dst in absent:
        @pl.when(gone)
        def _(dst=dst):
            dst[...] = jnp.zeros(dst.shape, jnp.float32)
    for c in range(2):
        for z in range(layers):
            summed = flat[c, z, pl.ds(0, rows)]
            for m in range(1, members):
                summed = summed + flat[2 * m + c, z, pl.ds(0, rows)]
            w_core[c, z] = cover_core * summed

    peer = {"ens": lax.rem(ie + 1, ne)}

    def to_peer(src, dst):
        return pltpu.make_async_remote_copy(
            src_ref=src, dst_ref=dst, send_sem=peer_send, recv_sem=peer_recv,
            device_id=peer, device_id_type=mesh_id)

    send_w = to_peer(w_core, w_peer)
    send_r = [to_peer(r_core.at[m], r_peer.at[m]) for m in range(members)]
    send_a = [to_peer(a_core.at[m], a_peer.at[m]) for m in range(members)]
    send_w.start()

    def relay_wait(k):
        pl.semaphore_wait(relay.at[k], wide_count if k else near_count)

    def relay_on(k):
        relay_wait(k - 1)
        signal(relay.at[k], True)

    if rounds > 1:
        relay_on(1)
    late.wait()

    def at(ref, index, base, count=TALL):
        return jnp.concatenate([ref[index + (q, pl.ds(base, count))] for q in range(2)], axis=1)

    def put(ref, index, base, value):
        for q in range(2):
            ref[index + (q, pl.ds(base, value.shape[0]))] = value[:, cols * q:cols * (q + 1)]

    def assemble(k):
        settle([k], True)
        for i, place in enumerate(planes[k]):
            half = pl.ds(HALO * (i % 2), HALO)
            pair = pair_at[k] + i // 2
            flat[place + (pl.ds(rows, HALO),)] = below_r[pair, half]
            flat[place + (pl.ds(rows + HALO, HALO),)] = above_r[pair, half]
        for h in range(2):
            over = turn(corner_r[0, h, k], SPAN - rows)
            under = turn(corner_r[1, h, k], rows)
            start = TOP + cols if h else TOP - HALO
            for q in range(2):
                part = jnp.where(places(rows + HALO, cols * q), over, side_r[h, k, q])
                part = jnp.where(places(rows, cols * q), under, part)
                for n, f in enumerate(fields[k]):
                    tall[f, q, pl.ds(start, HALO)] = part[HALO * n:HALO * (n + 1)]
        for f in fields[k]:
            for q, half in enumerate(stood_up(f)):
                tall[f, q, pl.ds(TOP, cols)] = half

    def times(which, count, *makers):
        parts = []
        for start in range(0, count, STEP):
            for maker in makers:
                x = maker(start)
                high = x.astype(jnp.bfloat16)
                parts += [high, (x - high.astype(jnp.float32)).astype(jnp.bfloat16)]
        lhs = jnp.concatenate(parts, axis=0)
        outs = [jnp.dot(lhs, matrix[k], preferred_element_type=jnp.float32) for k in which]

        def piece(out, start, i):
            low = 2 * (start * len(makers) + STEP * i)
            return out[low:low + STEP] + out[low + STEP:low + 2 * STEP]

        return [(start, [[piece(out, start, i) for i in range(len(makers))] for out in outs])
                for start in range(0, count, STEP)]

    root_base, res_base, img_base = TOP - 3, TOP - 2, TOP - 1
    lane = iota((8, lanes), 1)
    layer = sum([(lane >= SPAN * z).astype(jnp.int32) for z in range(1, layers + 1)])
    place = lane - SPAN * layer
    inside = ((place < rows) & (layer < layers)).astype(jnp.float32)[0:1]

    def prepare():
        put(cover, (), root_base, jnp.dot(
            at(tall, (other,), root_base).astype(jnp.bfloat16), matrix[4],
            preferred_element_type=jnp.float32))

    def prepare_force():
        b = res_base
        row = (ix * rows + jnp.where(place < rows + HALO, place, place - SPAN))[0:1]
        thickness = 1.0 + 2.0 * row.astype(jnp.float32) / (np_ * rows - 1)

        def field(start):
            return at(tall, (other,), b + start, STEP)

        def across(start):
            return at(tall, (other,), b + start + 1, STEP) - at(tall, (other,), b + start - 1, STEP)

        frictions = range(7, 7 + members)
        for (start, first), (_, second) in zip(times((6, *frictions), TALL, field), times((5,), TALL, across)):
            covered = at(cover, (), b + start, STEP)
            here = pl.ds(start, STEP)
            force[0, here] = -(covered * thickness * (first[0][0] * 0.5))
            force[1, here] = -(covered * thickness * (second[0][0] * 0.5))
            for m in range(members):
                force[2 + m, here] = (1.0 - covered) + covered * first[1 + m][0]

    def roots_level(m):
        b = root_base

        def u(start, shift=0):
            return at(tall, (2 * m,), b + start + shift, STEP)

        def v(start, shift=0):
            return at(tall, (2 * m + 1,), b + start + shift, STEP)

        for start, ((u_i, v_i), (u_z, v_z)) in times((2, 3), TALL, u, v):
            u_j, v_j = u(start, 1) - u(start, -1), v(start, 1) - v(start, -1)
            shear = u_j + v_i
            strain = (4.0 * (u_i * (u_i + v_j) + v_j * v_j) + shear * shear
                      + (u_z * u_z + v_z * v_z)) * 0.0625
            root = at(cover, (), b + start, STEP) * jnp.exp(
                jnp.log(strain + 0.1) * (-1.0 / 6.0) + 0.5 * math.log(2.0))
            put(roots, (m,), b + start, root)
            put(pa, (m, 0), b + start, root * u(start))
            put(pa, (m, 1), b + start, root * v(start))

    def leaning(ref, index, base, c):
        def maker(start):
            low = base + start
            return at(ref, index, low, STEP) + STEP_J[c] * (
                at(ref, index, low - 1, STEP) + at(ref, index, low + 1, STEP))
        return maker

    def residual_level(m):
        b = res_base
        for c in range(2):
            for start, ((near, moved),) in times(
                    (c,), TALL, leaning(roots, (m,), b, c), leaning(pa, (m, c), b, c)):
                low, here = b + start, pl.ds(start, STEP)
                root = at(roots, (m,), low, STEP)
                weight = root * near + force[2 + m, here]
                r = force[c, here] - (weight * (at(cover, (), low, STEP) * at(tall, (2 * m + c,), low, STEP))
                                      - root * moved)
                put(tr, (m, c), low, weight)
                put(r_ext, (m, c), low, r)
                put(pb, (m, c), low, root * r)

    def image_level(m):
        b = img_base
        for c in range(2):
            for start, ((moved,),) in times((c,), TALL, leaning(pb, (m, c), b, c)):
                low = b + start
                root = at(roots, (m,), low, STEP)
                a = at(tr, (m, c), low, STEP) * at(r_ext, (m, c), low, STEP) - root * moved
                put(a_ext, (m, c), low, a)
                put(pa, (m, c), low, root * a)

    def second_level(m):
        sums = None
        for c in range(2):
            def scaled(start):
                return at(pa, (m, c), TOP + start, STEP)

            def one_way(start):
                return scaled(start) + (2.0 * STEP_J[c]) * at(pa, (m, c), TOP - 1 + start, STEP)

            for start, ((out,),) in times((c,), cols, one_way):
                low = TOP + start
                r, a = at(r_ext, (m, c), low, STEP), at(a_ext, (m, c), low, STEP)
                square = a * a
                terms = (r * r, r * a, square, at(tr, (m, c), low, STEP) * square - scaled(start) * out)
                sums = terms if sums is None else [s + t for s, t in zip(sums, terms)]
        return [inside * jnp.sum(s, axis=0, keepdims=True) for s in sums]

    grams = []
    assemble(0)
    prepare()
    prepare_force()
    for m in range(members):
        assemble(1 + m)
        roots_level(m)
        if m > 0:
            image_level(m - 1)
        residual_level(m)
        if m > 0:
            grams.append(second_level(m - 1))
        if m == 0:
            for k in range(2, rounds):
                relay_on(k)
    image_level(members - 1)
    grams.append(second_level(members - 1))

    lane_1 = iota((1, cols), 1)
    mine = jnp.zeros((1, cols), jnp.float32)
    for m in range(members):
        for q, acc in enumerate(grams[m]):
            mine = jnp.where(lane_1 == 4 * m + q, jnp.sum(acc, axis=1, keepdims=True), mine)
    gram_s[0] = mine

    if rounds > 0:
        relay_wait(rounds - 1)

    def send_gram(d):
        px, py, pe = group_place(d)
        copy = pltpu.make_async_remote_copy(
            src_ref=gram_s, dst_ref=gram_r.at[pl.ds(d, 1)],
            send_sem=gram_send, recv_sem=gram_recv,
            device_id={"plane": px, "planey": py, "ens": pe}, device_id_type=mesh_id)
        own = (px == ix) & (py == iy) & (pe == ie)
        pl.when(jnp.logical_not(own))(copy.start)

    each_peer(send_gram)
    own_place = lax.rem(2 * ix + 1, np_) * nq + lax.rem(2 * iy + 1, nq)
    gram_r[pl.ds(own_place, 1)] = mine[None]

    def lie_down(src, dst):
        for c in range(2):
            flat_rows = jnp.concatenate(
                [src[c, q, pl.ds(TOP, cols)].T for q in range(2)], axis=0)
            for z in range(layers):
                dst[c, z] = flat_rows[SPAN * z:SPAN * z + rows]

    for m in range(members):
        lie_down(r_ext.at[m], r_core.at[m])
        send_r[m].start()
        lie_down(a_ext.at[m], a_core.at[m])
        send_a[m].start()
    everything = pltpu.make_async_remote_copy(
        src_ref=gram_blank, dst_ref=gram_blank, send_sem=gram_send, recv_sem=gram_recv,
        device_id=peer, device_id_type=mesh_id)
    everything.wait_recv()

    half = np_ * nq
    sums = [jnp.sum(gram_r[half * e:half * (e + 1)], axis=0) for e in range(ne)]
    steps = []
    for e in range(ne):
        for m in range(members):
            g_rr, g_ra, g_aa, g_ab = [
                jnp.sum(jnp.where(lane_1 == 4 * m + q, sums[e], 0.0), axis=1, keepdims=True)
                for q in range(4)
            ]
            first_step = g_rr / g_ra
            following = g_rr - 2.0 * first_step * g_ra + first_step * first_step * g_aa
            growth = 1.0 + following / g_rr
            curve = (growth * growth * g_ra - 2.0 * growth * first_step * g_aa
                     + first_step * first_step * g_ab)
            second_step = following / curve
            share = 1.0 / (members * ne)
            steps.append(((first_step + second_step * growth) * share,
                          second_step * first_step * share))

    peer_part = wide_blank.at[pl.ds(0, 1 + 2 * members)]
    peer_bulk = to_peer(peer_part, peer_part)
    peer_bulk.wait_recv()
    share = 1.0 / (members * ne)

    def final_step(z, carry):
        for c in range(2):
            value = share * (w_core[c, z] + w_peer[c, z])
            for m in range(members):
                one, two = steps[m]
                value = value + one * r_core[m, c, z] - two * a_core[m, c, z]
                one, two = steps[members + m]
                value = value + one * r_peer[m, c, z] - two * a_peer[m, c, z]
            out_ref[c, z] = value
        return carry

    lax.fori_loop(0, layers, final_step, 0)

    settle(list(chunks), False)
    peer_bulk.wait_send()
    everything.wait_send()


def body(sizes, u_prior, friction_rows, friction_table, bed_fixed, ice_mask):
    members, _, layers, rows, cols = u_prior.shape
    levels = friction_table.shape[0]
    total = sizes[0] * sizes[1] * sizes[2]
    fixed = 2 + members
    pairs = (fixed + fixed % 2 + members * 2 * layers) // 2
    fields, lanes = 2 * members + 1, 2 * cols
    rounds = max(max(sizes[0], sizes[1]) - 2, 2)
    f32 = jnp.float32
    matrices = jnp.asarray(stencils(layers, members, lanes), jnp.bfloat16)
    any_space = pl.BlockSpec(memory_space=pl.ANY)
    vmem = lambda *shape: pltpu.VMEM(shape, f32)
    core = (members, 2, layers, rows, cols)
    tall = (2, PAD, cols)
    each = (members, 2) + tall
    inputs = (friction_rows, u_prior, friction_table, bed_fixed, ice_mask, matrices)
    return pl.pallas_call(
        functools.partial(kernel, sizes),
        out_shape=pltpu.VMEM((2, layers, rows, cols), f32),
        in_specs=[any_space] * 6,
        out_specs=pl.BlockSpec(memory_space=pltpu.VMEM),
        scratch_shapes=[
            pltpu.SMEM((members,), jnp.int32), vmem(fields, layers + 1, SPAN, cols),
            vmem(levels, rows, cols),
            pltpu.VMEM((rows, cols), jnp.int32), pltpu.VMEM((rows, cols), jnp.int32),
            pltpu.VMEM(matrices.shape, jnp.bfloat16),
            vmem(pairs, 8, cols), vmem(pairs, 8, cols),
            vmem(2, members + 1, 2, 8, cols), vmem(2, 2, members + 1, 8, cols),
            vmem(pairs, 8, cols), vmem(pairs, 8, cols),
            vmem(2, members + 1, 2, 8, cols), vmem(2, 2, members + 1, 8, cols),
            vmem(fields, *tall), vmem(*tall), vmem(members, *tall),
            vmem(*each), vmem(*each), vmem(*each), vmem(*each), vmem(*each),
            vmem(2 + members, TALL, lanes),
            vmem(*core[1:]), vmem(*core), vmem(*core), vmem(*core), vmem(*core), vmem(*core[1:]),
            vmem(1, 1, cols), vmem(total, 1, cols), vmem(total - 1, 1, cols), vmem(2 * pairs + 8 * (members + 1), 8, cols),
            vmem(1 + 2 * members, *core[1:]),
            pltpu.SemaphoreType.REGULAR((rounds,)),
            pltpu.SemaphoreType.DMA((members + 5,)),
            pltpu.SemaphoreType.DMA, pltpu.SemaphoreType.DMA((members + 1,)),
            pltpu.SemaphoreType.DMA, pltpu.SemaphoreType.DMA,
            pltpu.SemaphoreType.DMA, pltpu.SemaphoreType.DMA,
        ],
        compiler_params=pltpu.CompilerParams(
            collective_id=0, has_side_effects=True, vmem_limit_bytes=40 << 20),
        name="picard",
    )(*[pltpu.with_memory_space_constraint(x, pltpu.HBM) for x in inputs])


def solution(mesh):
    sizes = (mesh.shape["plane"], mesh.shape["planey"], mesh.shape["ens"])
    in_specs = (
        P(("group", "ens"), None, None, "plane", "planey"),
        P(("group", "ens")),
        P("group", "plane", "planey"),
        P("plane", "planey"),
        P("plane", "planey"),
    )
    out_specs = P("group", None, "plane", "planey")
    return jax.shard_map(functools.partial(body, sizes), mesh=mesh, in_specs=in_specs,
                         out_specs=out_specs, check_vma=False)
```

time: 17.1 us -> 15.9 us (0.930)
  Pallas kernels: 16.3 us -> 15.1 us
    pallas_call x1, Pallas kernels: 16.3 us -> 15.1 us  [body(): pl.pallas_call(functools.partial(kernel, sizes), out_shape=pltpu.VMEM((2,...]
where the time goes in v3:
time: 15.9 us; the launch traced here: 15.8 us
  Pallas kernels  15.1 us (95%)
  local copies, waits for them, and re-layouts  0.67 us (4%)
    pallas_call x1, Pallas kernels, body(): pl.pallas_call(functools.partial(kernel, sizes), out_shape=pltpu.VMEM((2,...  15.1 us
    unnamed x1, local copies, waits for them, and re-layouts  0.67 us

profile of v3, /device:TPU:0, one launch (start us, length us, event | category | flops | bytes accessed | tf_op | source)
XLA Modules:
  0.0 15.8 jit_solution(13817393442384023519)
XLA Ops:
  0.0 15.1 %picard.1 = f32[2,10,16,128]{3,2,1,0:T(8,128)S(1)} custom-call(s32[2]{0:T(128)} %rows_hbm.1, f32[2,2,10,16,128]{4,3,2,1,0:T(8,128)} %u_hbm.1, f32[16,16,128]{2,1,0:T(8,128)} %table_hbm.1, s32[16,128]{1,0:T(8,128)} %bed_hbm.1, s32[16,128]{1,0:T(8,128)} %mask_hbm.1, bf16[9,256,256]{2,1,0:T(8,128)(2,1)} %constant.2.clone.matrix_hbm), custom_call_target="tpu_custom_call" | custom-call | tf_op jit(solution)/shard_map/picard/pallas_call | solution.py:542
  15.1 0.7 %copy.8 = f32[2,10,16,128]{3,2,1,0:T(8,128)} copy(f32[2,10,16,128]{3,2,1,0:T(8,128)S(1)} %picard.1) | data formatting | bytes 327680

commit v4 on v3

--- a/solution.py
+++ b/solution.py
@@ -27,7 +27,7 @@
     return pltpu.roll(x, step % x.shape[1], 1)
 
 
-def stencils(layers, members, lanes):
+def stencils(layers, lanes):
     def matrix(entry):
         out = np.zeros((lanes, lanes), np.float32)
         for z in range(layers):
@@ -51,9 +51,7 @@
     every = range(layers)
     out = [matrix(lambda dz, di, c=c: (2.0 - abs(dz)) * (STEP_I[c] if di else 1.0)) for c in range(2)]
     out.append(matrix(lambda dz, di: 0.0 if dz else float(di)))
-    out.append(matrix(lambda dz, di: 0.0 if di else float(dz)))
     out += [copies(1, every, same), copies(0, every, same), copies(0, every, difference)]
-    out += [copies(2 + m, (0,), same) for m in range(members)]
     return np.stack(out)
 
 
@@ -61,18 +59,20 @@
            rows_ref, flat, table_v, bed_v, mask_v, matrix,
            up_s, down_s, side_s, corner_s,
            below_r, above_r, side_r, corner_r,
-           tall, cover, roots, tr, pa, pb, r_ext, a_ext, force,
+           steep, tall, tall_steep, cover, roots, tr, pa, pb, r_ext, a_ext, force,
            w_core, r_core, a_core, r_peer, a_peer, w_peer, gram_s, gram_r, gram_blank, blank, wide_blank,
-           relay, in_sem, halo_send, halo_recv, peer_send, peer_recv, gram_send, gram_recv):
+           relay, in_sem, halo_recv, peer_recv, gram_recv):
     np_, nq, ne = sizes
-    members, _, layers, rows, cols = u_hbm.shape
+    other, layers, rows, cols = u_hbm.shape
+    members = other // 2
     ix, iy, ie = lax.axis_index("plane"), lax.axis_index("planey"), lax.axis_index("ens")
     total = np_ * nq * ne
     mesh_id = pl.DeviceIdType.MESH
     fixed = 2 + members
     lanes = 2 * cols
-    assert rows + 2 * HALO == SPAN and cols == 128 and layers * SPAN <= lanes and fixed <= layers
-    other = 2 * members
+    assert rows + 2 * HALO == SPAN and cols == 128 and layers * SPAN <= lanes
+    assert fixed <= layers and fixed * SPAN <= cols
+    halo_send, peer_send, gram_send = in_sem.at[0], in_sem.at[1], in_sem.at[2]
 
     reach = max(np_, nq)
     rounds = reach - 2 if reach > 3 else reach - 1
@@ -107,10 +107,9 @@
     loads = [
         pltpu.make_async_copy(src, dst, in_sem.at[i])
         for i, (src, dst) in enumerate(
-            [(u_hbm.at[m], flat.at[pl.ds(2 * m, 2), pl.ds(0, layers), pl.ds(0, rows)])
-             for m in range(members)]
-            + [(table_hbm, table_v), (bed_hbm, bed_v), (mask_hbm, mask_v), (rows_hbm, rows_ref),
-               (matrix_hbm, matrix)])
+            ((u_hbm, flat.at[pl.ds(0, other), pl.ds(0, layers), pl.ds(0, rows)]),
+             (table_hbm, table_v), (bed_hbm, bed_v), (mask_hbm, mask_v), (rows_hbm, rows_ref),
+             (matrix_hbm, matrix)))
     ]
     for load in loads:
         load.start()
@@ -217,18 +216,18 @@
                 out = here if out is None else out | here
         return out
 
-    def stood_up(f):
-        plain = flat[f].reshape((layers + 1) * SPAN, cols)
+    def stood_up(field):
+        plain = field[...].reshape((layers + 1) * SPAN, cols)
         return [plain[cols * h:cols * (h + 1)].T for h in range(2)]
 
-    for k in chunks:
+    def pack(k):
         for i, at in enumerate(planes[k]):
             half = pl.ds(HALO * (i % 2), HALO)
             up_s[pair_at[k] + i // 2, half] = flat[at + (pl.ds(0, HALO),)]
             down_s[pair_at[k] + i // 2, half] = flat[at + (pl.ds(rows - HALO, HALO),)]
         edges = []
         for f in fields[k]:
-            halves = stood_up(f)
+            halves = stood_up(flat.at[f])
             edges.append([[half[start:start + HALO] for half in halves] for start in (0, cols - HALO)])
         if len(edges) == 1:
             edges.append([[jnp.zeros((HALO, cols), jnp.float32)] * 2] * 2)
@@ -239,10 +238,18 @@
             corner_s[0, h, k] = jnp.where(places(0, 0), pair[0], pair[1])
             corner_s[1, h, k] = jnp.where(places(rows - HALO, 0), pair[0], pair[1])
 
+    def send(k):
+        for to_ok, copy in flows[k]:
+            pl.when(to_ok)(copy.start)
+
+    pack(0)
+    pack(1)
     pl.semaphore_wait(barrier, near_count)
-    for chunk in flows:
-        for to_ok, copy in chunk:
-            pl.when(to_ok)(copy.start)
+    send(0)
+    send(1)
+    for k in chunks[2:]:
+        pack(k)
+        send(k)
     if rounds > 0:
         signal(relay.at[0], False)
 
@@ -287,8 +294,23 @@
         for q in range(2):
             ref[index + (q, pl.ds(base, value.shape[0]))] = value[:, cols * q:cols * (q + 1)]
 
+    def steepen(m, part):
+        for z in range(layers):
+            square = None
+            for f in (2 * m, 2 * m + 1):
+                change = None
+                if z < layers - 1:
+                    change = flat[f, z + 1, part]
+                if z > 0:
+                    change = flat[f, z - 1, part] if change is None else change - flat[f, z - 1, part]
+                square = change * change if square is None else square + change * change
+            steep[m, z, part] = square
+
+    for m in range(members):
+        steep[m, layers] = jnp.zeros((SPAN, cols), jnp.float32)
+        steepen(m, pl.ds(0, rows))
+
     def assemble(k):
-        settle([k], True)
         for i, place in enumerate(planes[k]):
             half = pl.ds(HALO * (i % 2), HALO)
             pair = pair_at[k] + i // 2
@@ -298,14 +320,30 @@
             over = turn(corner_r[0, h, k], SPAN - rows)
             under = turn(corner_r[1, h, k], rows)
             start = TOP + cols if h else TOP - HALO
+            parts = []
             for q in range(2):
                 part = jnp.where(places(rows + HALO, cols * q), over, side_r[h, k, q])
                 part = jnp.where(places(rows, cols * q), under, part)
                 for n, f in enumerate(fields[k]):
                     tall[f, q, pl.ds(start, HALO)] = part[HALO * n:HALO * (n + 1)]
+                parts.append(part)
+            if k:
+                uppers, lowers = [turn(p, -SPAN) for p in parts], [turn(p, SPAN) for p in parts]
+                for q in range(2):
+                    whole = lane8 + cols * q
+                    upper = jnp.where(lane8 < cols - SPAN, uppers[q], uppers[1 - q])
+                    lower = jnp.where(lane8 >= SPAN, lowers[q], lowers[1 - q])
+                    change = (jnp.where(whole < (layers - 1) * SPAN, upper, 0.0)
+                              - jnp.where(whole >= SPAN, lower, 0.0))
+                    change = change * change
+                    tall_steep[k - 1, q, pl.ds(start, HALO)] = change[0:HALO] + change[HALO:2 * HALO]
         for f in fields[k]:
-            for q, half in enumerate(stood_up(f)):
+            for q, half in enumerate(stood_up(flat.at[f])):
                 tall[f, q, pl.ds(TOP, cols)] = half
+        if k:
+            steepen(k - 1, pl.ds(rows, SPAN - rows))
+            for q, half in enumerate(stood_up(steep.at[k - 1])):
+                tall_steep[k - 1, q, pl.ds(TOP, cols)] = half
 
     def times(which, count, *makers):
         parts = []
@@ -332,7 +370,7 @@
 
     def prepare():
         put(cover, (), root_base, jnp.dot(
-            at(tall, (other,), root_base).astype(jnp.bfloat16), matrix[4],
+            at(tall, (other,), root_base).astype(jnp.bfloat16), matrix[3],
             preferred_element_type=jnp.float32))
 
     def prepare_force():
@@ -346,14 +384,20 @@
         def across(start):
             return at(tall, (other,), b + start + 1, STEP) - at(tall, (other,), b + start - 1, STEP)
 
-        frictions = range(7, 7 + members)
-        for (start, first), (_, second) in zip(times((6, *frictions), TALL, field), times((5,), TALL, across)):
+        firsts, seconds = times((5,), TALL, field), times((4,), TALL, across)
+        ground = iota((STEP, cols), 1) < SPAN
+        yield
+        for (start, first), (_, second) in zip(firsts, seconds):
             covered = at(cover, (), b + start, STEP)
             here = pl.ds(start, STEP)
             force[0, here] = -(covered * thickness * (first[0][0] * 0.5))
             force[1, here] = -(covered * thickness * (second[0][0] * 0.5))
             for m in range(members):
-                force[2 + m, here] = (1.0 - covered) + covered * first[1 + m][0]
+                rub = turn(tall[other, 0, pl.ds(b + start, STEP)], -SPAN * (2 + m))
+                rub = jnp.where(ground, covered[:, 0:cols] * rub, 0.0)
+                dry = 1.0 - covered
+                force[2 + m, here] = jnp.concatenate([dry[:, 0:cols] + rub, dry[:, cols:]], axis=1)
+            yield
 
     def roots_level(m):
         b = root_base
@@ -364,16 +408,19 @@
         def v(start, shift=0):
             return at(tall, (2 * m + 1,), b + start + shift, STEP)
 
-        for start, ((u_i, v_i), (u_z, v_z)) in times((2, 3), TALL, u, v):
+        products = times((2,), TALL, u, v)
+        yield
+        for start, ((u_i, v_i),) in products:
             u_j, v_j = u(start, 1) - u(start, -1), v(start, 1) - v(start, -1)
             shear = u_j + v_i
             strain = (4.0 * (u_i * (u_i + v_j) + v_j * v_j) + shear * shear
-                      + (u_z * u_z + v_z * v_z)) * 0.0625
+                      + at(tall_steep, (m,), b + start, STEP)) * 0.0625
             root = at(cover, (), b + start, STEP) * jnp.exp(
                 jnp.log(strain + 0.1) * (-1.0 / 6.0) + 0.5 * math.log(2.0))
             put(roots, (m,), b + start, root)
             put(pa, (m, 0), b + start, root * u(start))
             put(pa, (m, 1), b + start, root * v(start))
+            yield
 
     def leaning(ref, index, base, c):
         def maker(start):
@@ -384,9 +431,12 @@
 
     def residual_level(m):
         b = res_base
+        products = []
         for c in range(2):
-            for start, ((near, moved),) in times(
-                    (c,), TALL, leaning(roots, (m,), b, c), leaning(pa, (m, c), b, c)):
+            products.append(times((c,), TALL, leaning(roots, (m,), b, c), leaning(pa, (m, c), b, c)))
+            yield
+        for steps_of in zip(*products):
+            for c, (start, ((near, moved),)) in enumerate(steps_of):
                 low, here = b + start, pl.ds(start, STEP)
                 root = at(roots, (m,), low, STEP)
                 weight = root * near + force[2 + m, here]
@@ -395,51 +445,71 @@
                 put(tr, (m, c), low, weight)
                 put(r_ext, (m, c), low, r)
                 put(pb, (m, c), low, root * r)
+            yield
 
     def image_level(m):
         b = img_base
+        products = []
         for c in range(2):
-            for start, ((moved,),) in times((c,), TALL, leaning(pb, (m, c), b, c)):
+            products.append(times((c,), TALL, leaning(pb, (m, c), b, c)))
+            yield
+        for steps_of in zip(*products):
+            for c, (start, ((moved,),)) in enumerate(steps_of):
                 low = b + start
                 root = at(roots, (m,), low, STEP)
                 a = at(tr, (m, c), low, STEP) * at(r_ext, (m, c), low, STEP) - root * moved
                 put(a_ext, (m, c), low, a)
                 put(pa, (m, c), low, root * a)
+            yield
+
+    grams = [None] * members
 
     def second_level(m):
+        def one_way(c):
+            def maker(start):
+                low = TOP + start
+                return at(pa, (m, c), low, STEP) + (2.0 * STEP_J[c]) * at(pa, (m, c), low - 1, STEP)
+            return maker
+
+        products = []
+        for c in range(2):
+            products.append(times((c,), cols, one_way(c)))
+            yield
         sums = None
-        for c in range(2):
-            def scaled(start):
-                return at(pa, (m, c), TOP + start, STEP)
-
-            def one_way(start):
-                return scaled(start) + (2.0 * STEP_J[c]) * at(pa, (m, c), TOP - 1 + start, STEP)
-
-            for start, ((out,),) in times((c,), cols, one_way):
+        for steps_of in zip(*products):
+            for c, (start, ((out,),)) in enumerate(steps_of):
                 low = TOP + start
                 r, a = at(r_ext, (m, c), low, STEP), at(a_ext, (m, c), low, STEP)
                 square = a * a
-                terms = (r * r, r * a, square, at(tr, (m, c), low, STEP) * square - scaled(start) * out)
+                terms = (r * r, r * a, square,
+                         at(tr, (m, c), low, STEP) * square - at(pa, (m, c), low, STEP) * out)
                 sums = terms if sums is None else [s + t for s, t in zip(sums, terms)]
-        return [inside * jnp.sum(s, axis=0, keepdims=True) for s in sums]
-
-    grams = []
+            yield
+        grams[m] = [inside * jnp.sum(s, axis=0, keepdims=True) for s in sums]
+
+    def together(*levels):
+        levels = list(levels)
+        while levels:
+            for level in list(levels):
+                try:
+                    next(level)
+                except StopIteration:
+                    levels.remove(level)
+
+    settle([0], True)
+    settle([1], True)
     assemble(0)
+    assemble(1)
     prepare()
-    prepare_force()
-    for m in range(members):
-        assemble(1 + m)
-        roots_level(m)
-        if m > 0:
-            image_level(m - 1)
-        residual_level(m)
-        if m > 0:
-            grams.append(second_level(m - 1))
-        if m == 0:
-            for k in range(2, rounds):
-                relay_on(k)
-    image_level(members - 1)
-    grams.append(second_level(members - 1))
+    together(roots_level(0), prepare_force())
+    for k in range(2, rounds):
+        relay_on(k)
+    stages = (roots_level, residual_level, image_level, second_level)
+    for turn_of in range(1, members + len(stages) - 1):
+        if turn_of < members:
+            settle([1 + turn_of], True)
+            assemble(1 + turn_of)
+        together(*[stages[turn_of - m](m) for m in range(members) if 0 <= turn_of - m < len(stages)])
 
     lane_1 = iota((1, cols), 1)
     mine = jnp.zeros((1, cols), jnp.float32)
@@ -505,7 +575,7 @@
     peer_bulk.wait_recv()
     share = 1.0 / (members * ne)
 
-    def final_step(z, carry):
+    def final_step(z):
         for c in range(2):
             value = share * (w_core[c, z] + w_peer[c, z])
             for m in range(members):
@@ -514,9 +584,9 @@
                 one, two = steps[members + m]
                 value = value + one * r_peer[m, c, z] - two * a_peer[m, c, z]
             out_ref[c, z] = value
-        return carry
-
-    lax.fori_loop(0, layers, final_step, 0)
+
+    for z in range(layers):
+        final_step(z)
 
     settle(list(chunks), False)
     peer_bulk.wait_send()
@@ -532,13 +602,13 @@
     fields, lanes = 2 * members + 1, 2 * cols
     rounds = max(max(sizes[0], sizes[1]) - 2, 2)
     f32 = jnp.float32
-    matrices = jnp.asarray(stencils(layers, members, lanes), jnp.bfloat16)
+    matrices = jnp.asarray(stencils(layers, lanes), jnp.bfloat16)
     any_space = pl.BlockSpec(memory_space=pl.ANY)
     vmem = lambda *shape: pltpu.VMEM(shape, f32)
     core = (members, 2, layers, rows, cols)
     tall = (2, PAD, cols)
     each = (members, 2) + tall
-    inputs = (friction_rows, u_prior, friction_table, bed_fixed, ice_mask, matrices)
+    inputs = (friction_rows, u_prior.reshape((-1,) + u_prior.shape[2:]), friction_table, bed_fixed, ice_mask, matrices)
     return pl.pallas_call(
         functools.partial(kernel, sizes),
         out_shape=pltpu.VMEM((2, layers, rows, cols), f32),
@@ -553,17 +623,16 @@
             vmem(2, members + 1, 2, 8, cols), vmem(2, 2, members + 1, 8, cols),
             vmem(pairs, 8, cols), vmem(pairs, 8, cols),
             vmem(2, members + 1, 2, 8, cols), vmem(2, 2, members + 1, 8, cols),
-            vmem(fields, *tall), vmem(*tall), vmem(members, *tall),
+            vmem(members, layers + 1, SPAN, cols), vmem(fields, *tall), vmem(members, *tall),
+            vmem(*tall), vmem(members, *tall),
             vmem(*each), vmem(*each), vmem(*each), vmem(*each), vmem(*each),
             vmem(2 + members, TALL, lanes),
             vmem(*core[1:]), vmem(*core), vmem(*core), vmem(*core), vmem(*core), vmem(*core[1:]),
             vmem(1, 1, cols), vmem(total, 1, cols), vmem(total - 1, 1, cols), vmem(2 * pairs + 8 * (members + 1), 8, cols),
             vmem(1 + 2 * members, *core[1:]),
             pltpu.SemaphoreType.REGULAR((rounds,)),
-            pltpu.SemaphoreType.DMA((members + 5,)),
-            pltpu.SemaphoreType.DMA, pltpu.SemaphoreType.DMA((members + 1,)),
-            pltpu.SemaphoreType.DMA, pltpu.SemaphoreType.DMA,
-            pltpu.SemaphoreType.DMA, pltpu.SemaphoreType.DMA,
+            pltpu.SemaphoreType.DMA((6,)),
+            pltpu.SemaphoreType.DMA((members + 1,)), pltpu.SemaphoreType.DMA, pltpu.SemaphoreType.DMA,
         ],
         compiler_params=pltpu.CompilerParams(
             collective_id=0, has_side_effects=True, vmem_limit_bytes=40 << 20),

time: 15.9 us -> 15.4 us (0.969)
  Pallas kernels: 15.1 us -> 14.5 us
    pallas_call x1, Pallas kernels: 15.1 us -> 14.5 us  [body(): pl.pallas_call(functools.partial(kernel, sizes), out_shape=pltpu.VMEM((2,...]
where the time goes in v4:
time: 15.4 us; the launch traced here: 15.2 us
  Pallas kernels  14.5 us (94%)
  local copies, waits for them, and re-layouts  0.67 us (4%)
    pallas_call x1, Pallas kernels, body(): pl.pallas_call(functools.partial(kernel, sizes), out_shape=pltpu.VMEM((2,...  14.5 us
    unnamed x1, local copies, waits for them, and re-layouts  0.67 us

profile of v4, /device:TPU:0, one launch (start us, length us, event | category | flops | bytes accessed | tf_op | source)
XLA Modules:
  0.0 15.2 jit_solution(7612334071776319990)
XLA Ops:
  0.0 14.5 %picard.1 = f32[2,10,16,128]{3,2,1,0:T(8,128)S(1)} custom-call(s32[2]{0:T(128)} %rows_hbm.1, f32[4,10,16,128]{3,2,1,0:T(8,128)} %bitcast.1, f32[16,16,128]{2,1,0:T(8,128)} %table_hbm.1, s32[16,128]{1,0:T(8,128)} %bed_hbm.1, s32[16,128]{1,0:T(8,128)} %mask_hbm.1, bf16[6,256,256]{2,1,0:T(8,128)(2,1)} %constant.2.clone.matrix_hbm), custom_call_target="tpu_custom_call" | custom-call | tf_op jit(solution)/shard_map/picard/pallas_call | solution.py:612
  14.6 0.7 %copy.8 = f32[2,10,16,128]{3,2,1,0:T(8,128)} copy(f32[2,10,16,128]{3,2,1,0:T(8,128)S(1)} %picard.1) | data formatting | bytes 327680

commit v5 on v4

--- a/solution.py
+++ b/solution.py
@@ -12,7 +12,7 @@
 HALO = 4
 TOP = 8
 SPAN = 24
-TALL = 144
+TALL = 136
 PAD = 160
 STEP = 16
 STEP_I = (0.25, 0.125)
@@ -111,9 +111,9 @@
              (table_hbm, table_v), (bed_hbm, bed_v), (mask_hbm, mask_v), (rows_hbm, rows_ref),
              (matrix_hbm, matrix)))
     ]
+    late = loads.pop()
     for load in loads:
         load.start()
-    late = loads.pop()
 
     def group_place(d):
         de, rest = d // (np_ * nq), d % (np_ * nq)
@@ -199,6 +199,7 @@
 
     for load in loads:
         load.wait()
+    late.start()
 
     cover_core = mask_v[...].astype(jnp.float32)
     flat[other, 0, pl.ds(0, rows)] = bed_v[...].astype(jnp.float32) * bed_unit
@@ -345,22 +346,27 @@
             for q, half in enumerate(stood_up(steep.at[k - 1])):
                 tall_steep[k - 1, q, pl.ds(TOP, cols)] = half
 
-    def times(which, count, *makers):
-        parts = []
-        for start in range(0, count, STEP):
-            for maker in makers:
-                x = maker(start)
-                high = x.astype(jnp.bfloat16)
-                parts += [high, (x - high.astype(jnp.float32)).astype(jnp.bfloat16)]
-        lhs = jnp.concatenate(parts, axis=0)
-        outs = [jnp.dot(lhs, matrix[k], preferred_element_type=jnp.float32) for k in which]
-
-        def piece(out, start, i):
-            low = 2 * (start * len(makers) + STEP * i)
-            return out[low:low + STEP] + out[low + STEP:low + 2 * STEP]
-
-        return [(start, [[piece(out, start, i) for i in range(len(makers))] for out in outs])
-                for start in range(0, count, STEP)]
+    def times(count, *jobs):
+        steps_of = [(start, min(STEP, count - start)) for start in range(0, count, STEP)]
+        parts = [[] for _ in jobs]
+        for start, n in steps_of:
+            for (_, makers), part in zip(jobs, parts):
+                for maker in makers:
+                    x = maker(start, n)
+                    high = x.astype(jnp.bfloat16)
+                    low = x - high.astype(jnp.float32)
+                    if n == STEP:
+                        part += [high, low.astype(jnp.bfloat16)]
+                    else:
+                        part.append(jnp.concatenate([x, low], axis=0).astype(jnp.bfloat16))
+        outs = [jnp.dot(jnp.concatenate(part, axis=0), matrix[k], preferred_element_type=jnp.float32)
+                for (k, _), part in zip(jobs, parts)]
+
+        def piece(out, low, n):
+            return out[low:low + n] + out[low + n:low + 2 * n]
+
+        return [(start, n, [[piece(out, 2 * (start * len(makers) + n * i), n) for i in range(len(makers))]
+                            for (_, makers), out in zip(jobs, outs)]) for start, n in steps_of]
 
     root_base, res_base, img_base = TOP - 3, TOP - 2, TOP - 1
     lane = iota((8, lanes), 1)
@@ -370,7 +376,7 @@
 
     def prepare():
         put(cover, (), root_base, jnp.dot(
-            at(tall, (other,), root_base).astype(jnp.bfloat16), matrix[3],
+            at(tall, (other,), root_base, TALL + 8).astype(jnp.bfloat16), matrix[3],
             preferred_element_type=jnp.float32))
 
     def prepare_force():
@@ -378,69 +384,74 @@
         row = (ix * rows + jnp.where(place < rows + HALO, place, place - SPAN))[0:1]
         thickness = 1.0 + 2.0 * row.astype(jnp.float32) / (np_ * rows - 1)
 
-        def field(start):
-            return at(tall, (other,), b + start, STEP)
-
-        def across(start):
-            return at(tall, (other,), b + start + 1, STEP) - at(tall, (other,), b + start - 1, STEP)
-
-        firsts, seconds = times((5,), TALL, field), times((4,), TALL, across)
         ground = iota((STEP, cols), 1) < SPAN
+
+        def field(start, n):
+            return at(tall, (other,), b + start, n)
+
+        def across(start, n):
+            return at(tall, (other,), b + start + 1, n) - at(tall, (other,), b + start - 1, n)
+
+        products = times(TALL, (5, [field]), (4, [across]))
         yield
-        for (start, first), (_, second) in zip(firsts, seconds):
-            covered = at(cover, (), b + start, STEP)
-            here = pl.ds(start, STEP)
-            force[0, here] = -(covered * thickness * (first[0][0] * 0.5))
-            force[1, here] = -(covered * thickness * (second[0][0] * 0.5))
+        for start, n, ((slope_x,), (slope_y,)) in products:
+            covered = at(cover, (), b + start, n)
+            here = pl.ds(start, n)
+            force[0, here] = -(covered * thickness * (slope_x * 0.5))
+            force[1, here] = -(covered * thickness * (slope_y * 0.5))
+            dry = 1.0 - covered
             for m in range(members):
-                rub = turn(tall[other, 0, pl.ds(b + start, STEP)], -SPAN * (2 + m))
-                rub = jnp.where(ground, covered[:, 0:cols] * rub, 0.0)
-                dry = 1.0 - covered
+                rub = turn(tall[other, 0, pl.ds(b + start, n)], -SPAN * (2 + m))
+                rub = jnp.where(ground[0:n], covered[:, 0:cols] * rub, 0.0)
                 force[2 + m, here] = jnp.concatenate([dry[:, 0:cols] + rub, dry[:, cols:]], axis=1)
             yield
 
     def roots_level(m):
         b = root_base
 
-        def u(start, shift=0):
-            return at(tall, (2 * m,), b + start + shift, STEP)
-
-        def v(start, shift=0):
-            return at(tall, (2 * m + 1,), b + start + shift, STEP)
-
-        products = times((2,), TALL, u, v)
+        def u(start, n, shift=0):
+            return at(tall, (2 * m,), b + start + shift, n)
+
+        def v(start, n, shift=0):
+            return at(tall, (2 * m + 1,), b + start + shift, n)
+
+        products = times(TALL, (2, [u, v]))
         yield
-        for start, ((u_i, v_i),) in products:
-            u_j, v_j = u(start, 1) - u(start, -1), v(start, 1) - v(start, -1)
+        for start, n, ((u_i, v_i),) in products:
+            u_j, v_j = u(start, n, 1) - u(start, n, -1), v(start, n, 1) - v(start, n, -1)
             shear = u_j + v_i
             strain = (4.0 * (u_i * (u_i + v_j) + v_j * v_j) + shear * shear
-                      + at(tall_steep, (m,), b + start, STEP)) * 0.0625
-            root = at(cover, (), b + start, STEP) * jnp.exp(
-                jnp.log(strain + 0.1) * (-1.0 / 6.0) + 0.5 * math.log(2.0))
+                      + (at(tall_steep, (m,), b + start, n) + 1.6))
+            root = at(cover, (), b + start, n) * jnp.exp2(
+                jnp.log(strain) * (-1.0 / (6.0 * math.log(2.0))) + (0.5 + 4.0 / 6.0))
             put(roots, (m,), b + start, root)
-            put(pa, (m, 0), b + start, root * u(start))
-            put(pa, (m, 1), b + start, root * v(start))
+            put(pa, (m, 0), b + start, root * u(start, n))
+            put(pa, (m, 1), b + start, root * v(start, n))
             yield
 
-    def leaning(ref, index, base, c):
-        def maker(start):
+    def leaning(ref, index, base, steps, known=None):
+        def maker(start, n):
             low = base + start
-            return at(ref, index, low, STEP) + STEP_J[c] * (
-                at(ref, index, low - 1, STEP) + at(ref, index, low + 1, STEP))
+            found = None if known is None else known.pop(start, None)
+            if found is None:
+                found = at(ref, index, low, n), at(ref, index, low - 1, n) + at(ref, index, low + 1, n)
+                if known is not None:
+                    known[start] = found
+            return found[0] + steps * found[1]
         return maker
 
     def residual_level(m):
-        b = res_base
-        products = []
-        for c in range(2):
-            products.append(times((c,), TALL, leaning(roots, (m,), b, c), leaning(pa, (m, c), b, c)))
-            yield
-        for steps_of in zip(*products):
-            for c, (start, ((near, moved),)) in enumerate(steps_of):
-                low, here = b + start, pl.ds(start, STEP)
-                root = at(roots, (m,), low, STEP)
+        b, known = res_base, {}
+        products = times(TALL, *[
+            (c, [leaning(roots, (m,), b, STEP_J[c], known), leaning(pa, (m, c), b, STEP_J[c])])
+            for c in range(2)])
+        yield
+        for start, n, pairs in products:
+            for c, (near, moved) in enumerate(pairs):
+                low, here = b + start, pl.ds(start, n)
+                root = at(roots, (m,), low, n)
                 weight = root * near + force[2 + m, here]
-                r = force[c, here] - (weight * (at(cover, (), low, STEP) * at(tall, (2 * m + c,), low, STEP))
+                r = force[c, here] - (weight * (at(cover, (), low, n) * at(tall, (2 * m + c,), low, n))
                                       - root * moved)
                 put(tr, (m, c), low, weight)
                 put(r_ext, (m, c), low, r)
@@ -449,15 +460,13 @@
 
     def image_level(m):
         b = img_base
-        products = []
-        for c in range(2):
-            products.append(times((c,), TALL, leaning(pb, (m, c), b, c)))
-            yield
-        for steps_of in zip(*products):
-            for c, (start, ((moved,),)) in enumerate(steps_of):
+        products = times(TALL, *[(c, [leaning(pb, (m, c), b, STEP_J[c])]) for c in range(2)])
+        yield
+        for start, n, pairs in products:
+            for c, (moved,) in enumerate(pairs):
                 low = b + start
-                root = at(roots, (m,), low, STEP)
-                a = at(tr, (m, c), low, STEP) * at(r_ext, (m, c), low, STEP) - root * moved
+                root = at(roots, (m,), low, n)
+                a = at(tr, (m, c), low, n) * at(r_ext, (m, c), low, n) - root * moved
                 put(a_ext, (m, c), low, a)
                 put(pa, (m, c), low, root * a)
             yield
@@ -466,23 +475,21 @@
 
     def second_level(m):
         def one_way(c):
-            def maker(start):
+            def maker(start, n):
                 low = TOP + start
-                return at(pa, (m, c), low, STEP) + (2.0 * STEP_J[c]) * at(pa, (m, c), low - 1, STEP)
+                return at(pa, (m, c), low, n) + (2.0 * STEP_J[c]) * at(pa, (m, c), low - 1, n)
             return maker
 
-        products = []
-        for c in range(2):
-            products.append(times((c,), cols, one_way(c)))
-            yield
+        products = times(cols, *[(c, [one_way(c)]) for c in range(2)])
+        yield
         sums = None
-        for steps_of in zip(*products):
-            for c, (start, ((out,),)) in enumerate(steps_of):
+        for start, n, pairs in products:
+            for c, (out,) in enumerate(pairs):
                 low = TOP + start
-                r, a = at(r_ext, (m, c), low, STEP), at(a_ext, (m, c), low, STEP)
+                r, a = at(r_ext, (m, c), low, n), at(a_ext, (m, c), low, n)
                 square = a * a
                 terms = (r * r, r * a, square,
-                         at(tr, (m, c), low, STEP) * square - at(pa, (m, c), low, STEP) * out)
+                         at(tr, (m, c), low, n) * square - at(pa, (m, c), low, n) * out)
                 sums = terms if sums is None else [s + t for s, t in zip(sums, terms)]
             yield
         grams[m] = [inside * jnp.sum(s, axis=0, keepdims=True) for s in sums]

time: 15.4 us -> 15.3 us (level)
  no operation moved by 1% of the time
where the time goes in v5:
time: 15.3 us; the launch traced here: 15.2 us
  Pallas kernels  14.5 us (95%)
  local copies, waits for them, and re-layouts  0.67 us (4%)
    pallas_call x1, Pallas kernels, body(): pl.pallas_call(functools.partial(kernel, sizes), out_shape=pltpu.VMEM((2,...  14.5 us
    unnamed x1, local copies, waits for them, and re-layouts  0.67 us

profile of v5, /device:TPU:0, one launch (start us, length us, event | category | flops | bytes accessed | tf_op | source)
XLA Modules:
  0.0 15.2 jit_solution(3257828411220098894)
XLA Ops:
  0.0 14.5 %picard.1 = f32[2,10,16,128]{3,2,1,0:T(8,128)S(1)} custom-call(s32[2]{0:T(128)} %rows_hbm.1, f32[4,10,16,128]{3,2,1,0:T(8,128)} %bitcast.1, f32[16,16,128]{2,1,0:T(8,128)} %table_hbm.1, s32[16,128]{1,0:T(8,128)} %bed_hbm.1, s32[16,128]{1,0:T(8,128)} %mask_hbm.1, bf16[6,256,256]{2,1,0:T(8,128)(2,1)} %constant.2.clone.matrix_hbm), custom_call_target="tpu_custom_call" | custom-call | tf_op jit(solution)/shard_map/picard/pallas_call | solution.py:619
  14.5 0.7 %copy.8 = f32[2,10,16,128]{3,2,1,0:T(8,128)} copy(f32[2,10,16,128]{3,2,1,0:T(8,128)S(1)} %picard.1) | data formatting | bytes 327680

commit v6 on v5

--- a/solution.py
+++ b/solution.py
@@ -513,6 +513,8 @@
         relay_on(k)
     stages = (roots_level, residual_level, image_level, second_level)
     for turn_of in range(1, members + len(stages) - 1):
+        if turn_of == 1 and rounds > 0:
+            relay_wait(rounds - 1)
         if turn_of < members:
             settle([1 + turn_of], True)
             assemble(1 + turn_of)
@@ -525,8 +527,6 @@
             mine = jnp.where(lane_1 == 4 * m + q, jnp.sum(acc, axis=1, keepdims=True), mine)
     gram_s[0] = mine
 
-    if rounds > 0:
-        relay_wait(rounds - 1)
 
     def send_gram(d):
         px, py, pe = group_place(d)
@@ -535,7 +535,10 @@
             send_sem=gram_send, recv_sem=gram_recv,
             device_id={"plane": px, "planey": py, "ens": pe}, device_id_type=mesh_id)
         own = (px == ix) & (py == iy) & (pe == ie)
-        pl.when(jnp.logical_not(own))(copy.start)
+        if isinstance(d, int) and d >= np_ * nq:
+            copy.start()
+        else:
+            pl.when(jnp.logical_not(own))(copy.start)
 
     each_peer(send_gram)
     own_place = lax.rem(2 * ix + 1, np_) * nq + lax.rem(2 * iy + 1, nq)

time: 15.3 us -> 15.3 us (level)
  no operation moved by 1% of the time
where the time goes in v6:
time: 15.3 us; the launch traced here: 15.2 us
  Pallas kernels  14.5 us (95%)
  local copies, waits for them, and re-layouts  0.67 us (4%)
    pallas_call x1, Pallas kernels, body(): pl.pallas_call(functools.partial(kernel, sizes), out_shape=pltpu.VMEM((2,...  14.5 us
    unnamed x1, local copies, waits for them, and re-layouts  0.67 us

profile of v6, /device:TPU:0, one launch (start us, length us, event | category | flops | bytes accessed | tf_op | source)
XLA Modules:
  0.0 15.2 jit_solution(5886740639597834683)
XLA Ops:
  0.0 14.5 %picard.1 = f32[2,10,16,128]{3,2,1,0:T(8,128)S(1)} custom-call(s32[2]{0:T(128)} %rows_hbm.1, f32[4,10,16,128]{3,2,1,0:T(8,128)} %bitcast.1, f32[16,16,128]{2,1,0:T(8,128)} %table_hbm.1, s32[16,128]{1,0:T(8,128)} %bed_hbm.1, s32[16,128]{1,0:T(8,128)} %mask_hbm.1, bf16[6,256,256]{2,1,0:T(8,128)(2,1)} %constant.2.clone.matrix_hbm), custom_call_target="tpu_custom_call" | custom-call | tf_op jit(solution)/shard_map/picard/pallas_call | solution.py:622
  14.5 0.7 %copy.8 = f32[2,10,16,128]{3,2,1,0:T(8,128)} copy(f32[2,10,16,128]{3,2,1,0:T(8,128)S(1)} %picard.1) | data formatting | bytes 327680
